TPU v7x, 512 devices: a whole 4x4x16 slice. The times are simulated.
512 devices in a mesh: freq: 8 (over y, z_hi), space: 64 (over z_lo, x, core).
Axes of the slice: x: 4, y: 4, z: 16 (z_hi: 2, z_lo: 8; z = z_hi * 8 + z_lo), core: 2. Of those that a mesh axis runs over, the one named last changes fastest.
Arguments:
- probes: float32 [2, 128, 128, 128], P(None, 'space'), may hold values from -6 to 6
- background: float32 [8, 2, 128, 128, 128], P('freq', None, 'space'), may hold values from -6 to 6
- medium: float32 [128, 128, 128], P('space'), may hold values from 0.5 to 2
- shifts: float32 [8, 2], P('freq'), may hold values from -1.25 to 1, as said below
- receivers: int32 [128, 128, 128], P('space'), may hold values 0 or 1
Outputs:
- hessian: float32 [2, 128, 128, 128], P(None, 'space', 'freq')
Inputs may be any that keep to these rules, and one draw needn't show every extreme that they name: `shifts`: column 0 lies in [-1.25, -0.5], column 1 in [0.2, 1.0].
All inputs are finite; a program needn't handle non-finite values. No bound on the sum of `receivers` on one device may be relied on, other than what follows from the above.
Results may differ from a plain program's by a relative error of at most 0.00002.
Values sent between devices are 32-bit elements; how exact they have to be, the bound alone decides.
No kernel may reach another device: no remote copies, remote signals or barrier semaphores. Data moves between devices by JAX's collectives and lax.ppermute only.
A program may use at most 64 MiB of HBM per device.

v0:
```python
import jax
import jax.numpy as jnp
from jax import lax
from jax.sharding import PartitionSpec as P

STEPS = 4


OMEGA_RELAX = 0.8


def padded(cells, sides, width):
    for axis, dim in sides:
        count = lax.axis_size(axis)
        ends = count - 1
        head = lax.slice_in_dim(cells, 0, width, axis=dim)
        tail = lax.slice_in_dim(cells, cells.shape[dim] - width, cells.shape[dim], axis=dim)
        cells = jnp.concatenate(
            [
                lax.ppermute(tail, axis, [(i, (i + 1) % count) for i in range(ends)]),
                cells,
                lax.ppermute(head, axis, [((i + 1) % count, i) for i in range(ends)]),
            ],
            axis=dim,
        )
    return cells


def in_blocks(shard, dim, length):
    before, after = (shard.shape[:dim], shard.shape[dim + 1 :])
    return jnp.moveaxis(shard.reshape(*before, length, -1, *after), dim, 0)


def summed_on_arrival(shard, axis, dim):
    parts = in_blocks(shard, dim, lax.axis_size(axis))
    arrived = lax.all_to_all(parts, axis, split_axis=0, concat_axis=0, tiled=True)
    return arrived.sum(axis=0)


def neighbours(extended):
    center = extended[:, :, 1:-1]
    beside_all = extended[:, :, 2:] + extended[:, :, :-2]
    pad_y_low = ((0, 0), (0, 0), (0, 0), (0, 1), (0, 0))
    pad_y_high = ((0, 0), (0, 0), (0, 0), (1, 0), (0, 0))
    pad_z_low = ((0, 0), (0, 0), (0, 0), (0, 0), (0, 1))
    pad_z_high = ((0, 0), (0, 0), (0, 0), (0, 0), (1, 0))
    beside_all = (
        beside_all
        + jnp.pad(center[:, :, :, 1:], pad_y_low)
        + jnp.pad(center[:, :, :, :-1], pad_y_high)
    )
    beside_all = (
        beside_all
        + jnp.pad(center[:, :, :, :, 1:], pad_z_low)
        + jnp.pad(center[:, :, :, :, :-1], pad_z_high)
    )
    return (center, beside_all)


def sweep_once(extended, factors, source):
    diag_re, diag_im, inv_re, inv_im = factors
    center, beside_all = neighbours(extended)
    resid_re = source[0] - (diag_re * center[0] - diag_im * center[1]) + beside_all[0]
    resid_im = source[1] - (diag_re * center[1] + diag_im * center[0]) + beside_all[1]
    return center + jnp.stack(
        [inv_re * resid_re - inv_im * resid_im, inv_re * resid_im + inv_im * resid_re]
    )


def coefficients(medium, shift_re, shift_im):
    diag_re = 6.0 + shift_re * medium
    diag_im = shift_im * medium
    denom = diag_re * diag_re + diag_im * diag_im
    return (diag_re, diag_im, OMEGA_RELAX * diag_re / denom, -OMEGA_RELAX * diag_im / denom)


def conjugate(factors):
    return (factors[0], -factors[1], factors[2], -factors[3])


def trimmed(factors, margin):
    return tuple((part[margin : part.shape[0] - margin] for part in factors))


def per_device(probes, background, medium, shifts, receivers):
    shift_re = shifts[0, 0]
    shift_im = shifts[0, 1]
    back_re = background[0, 0]
    back_im = background[0, 1]
    scaled_re = shift_re * back_re - shift_im * back_im
    scaled_im = shift_re * back_im + shift_im * back_re
    source = jnp.stack([scaled_re * probes, scaled_im * probes])
    listen = receivers.astype(jnp.float32)
    thickness = medium.shape[0]
    medium_wide = padded(medium, (("space", 0),), 2)
    factors = coefficients(medium_wide, shift_re, shift_im)
    position = lax.axis_index("space") * thickness + jnp.arange(thickness + 4, dtype=jnp.int32) - 2
    inside_all = ((position >= 0) & (position < thickness * lax.axis_size("space"))).astype(
        jnp.float32
    )
    inside = inside_all[1:-1][:, None, None]

    def relax_all(right_side, local_factors):
        side_wide = padded(right_side, (("space", 2),), 2)
        outer_factors = trimmed(local_factors, 1)
        inner_factors = trimmed(local_factors, 2)
        iterate = jnp.zeros(right_side.shape, jnp.float32)
        for repeat in range(STEPS // 2):
            extended = padded(iterate, (("space", 2),), 2)
            partial_sweep = sweep_once(extended, outer_factors, side_wide[:, :, 1:-1]) * inside
            iterate = sweep_once(partial_sweep, inner_factors, side_wide[:, :, 2:-2])
        return iterate

    forward = relax_all(source, factors)
    adjoint_field = relax_all(listen * forward, conjugate(factors))
    terms = scaled_re * adjoint_field[0] + scaled_im * adjoint_field[1]
    return summed_on_arrival(terms, "freq", 2)


def solution(mesh):
    in_specs = (
        P(None, "space", None, None),
        P("freq", None, "space", None, None),
        P("space", None, None),
        P("freq", None),
        P("space", None, None),
    )
    out_specs = P(None, "space", "freq", None)
    return jax.shard_map(
        per_device, mesh=mesh, in_specs=in_specs, out_specs=out_specs, check_vma=False
    )
```

profile of v0, /device:TPU:103, one launch (start us, length us, event | category | flops | bytes accessed | tf_op | source)
XLA Modules:
  0.0 130.0 jit_solution(16382373500466101155)
XLA Ops:
  0.0 5.4 %collective-permute-start = (f32[2,2,2,128,128]{4,3,2,1,0:T(8,128)S(1)}, f32[2,2,2,128,128]{4,3,2,1,0:T(8,128)S(1)}, u32[]{:S(2)}, u32[]{:S(2)}) collective-permute-start(f32[2,2,2,128,128]{4,3,2,1,0:T(8,128)S(1)} %broadcast.193), channel_id=1, source_target_pairs={{0,1},{1,2},{2,3},{3,4},{4,5},{5,6},{6,7},{7,8},{8,9},{9,10},{10,1... | collective-permute-start | bytes 1572872 | tf_op jit(solution)/shard_map/ppermute | solution.py:20
  5.4 1.9 %collective-permute-start.1 = (f32[2,2,2,128,128]{4,3,2,1,0:T(8,128)S(1)}, f32[2,2,2,128,128]{4,3,2,1,0:T(8,128)S(1)}, u32[]{:S(2)}, u32[]{:S(2)}) collective-permute-start(f32[2,2,2,128,128]{4,3,2,1,0:T(8,128)S(1)} %broadcast.193), channel_id=1, source_target_pairs={{1,0},{2,1},{3,2},{4,3},{5,4},{6,5},{7,6},{8,7},{9,8},{10,9},{11,1... | collective-permute-start | bytes 1572872 | tf_op jit(solution)/shard_map/ppermute | solution.py:22
  7.3 1.3 %fusion.54 = (f32[1,1]{1,0:T(1,128)}, f32[1,1]{1,0:T(1,128)}) fusion(f32[1,2]{1,0:T(1,128)} %param.8), kind=kLoop, calls=%fused_computation.127 | loop fusion | bytes 16 | tf_op jit(solution)/shard_map/slice | solution.py:87
  8.7 2.3 %multiply_subtract_fusion.6 = (f32[1,1,2,128,128]{4,3,2,1,0:T(8,128)S(1)}, f32[1,1,2,128,128]{4,3,2,1,0:T(8,128)S(1)}) fusion(f32[1,2,2,128,128]{4,3,2,1,0:T(8,128)} %param.6, f32[]{:T(128)} %bitcast.1, f32[]{:T(128)} %bitcast), kind=kLoop, calls=%fused_computation.104 | loop fusion | flops 196608 | bytes 524296 | tf_op jit(solution)/shard_map/sub | solution.py:90
  12.8 6.9 %collective-permute-start.4 = (f32[2,2,2,128,128]{4,3,2,1,0:T(8,128)}, f32[2,2,2,128,128]{4,3,2,1,0:T(8,128)S(1)}, u32[]{:S(2)}, u32[]{:S(2)}) collective-permute-start(f32[2,2,2,128,128]{4,3,2,1,0:T(8,128)} %pad_maximum_fusion.10), channel_id=1, source_target_pairs={{0,1},{1,2},{2,3},{3,4},{4,5},{5,6},{6,7},{7,8},{8,9},{9,10},{10,1... | collective-permute-start | bytes 1572872 | tf_op jit(solution)/shard_map/ppermute | solution.py:20
  19.7 1.9 %collective-permute-start.5 = (f32[2,2,2,128,128]{4,3,2,1,0:T(8,128)}, f32[2,2,2,128,128]{4,3,2,1,0:T(8,128)S(1)}, u32[]{:S(2)}, u32[]{:S(2)}) collective-permute-start(f32[2,2,2,128,128]{4,3,2,1,0:T(8,128)} %pad_maximum_fusion.10), channel_id=1, source_target_pairs={{1,0},{2,1},{3,2},{4,3},{5,4},{6,5},{7,6},{8,7},{9,8},{10,9},{11,1... | collective-permute-start | bytes 1572872 | tf_op jit(solution)/shard_map/ppermute | solution.py:22
  21.7 7.0 %collective-permute-start.2 = (f32[2,128,128]{2,1,0:T(8,128)S(1)}, f32[2,128,128]{2,1,0:T(8,128)}, u32[]{:S(2)}, u32[]{:S(2)}) collective-permute-start(f32[2,128,128]{2,1,0:T(8,128)S(1)} %copy-done.1), channel_id=1, source_target_pairs={{0,1},{1,2},{2,3},{3,4},{4,5},{5,6},{6,7},{7,8},{8,9},{9,10},{10,1... | collective-permute-start | bytes 393224 | tf_op jit(solution)/shard_map/ppermute | solution.py:20
  28.7 1.8 %collective-permute-done.2 = f32[2,128,128]{2,1,0:T(8,128)} collective-permute-done((f32[2,128,128]{2,1,0:T(8,128)S(1)}, f32[2,128,128]{2,1,0:T(8,128)}, u32[]{:S(2)}, u32[]{:S(2)}) %collective-permute-start.2) | collective-permute-done | bytes 131104 | tf_op jit(solution)/shard_map/ppermute | solution.py:20
  30.6 1.9 %collective-permute-start.3 = (f32[2,128,128]{2,1,0:T(8,128)S(1)}, f32[2,128,128]{2,1,0:T(8,128)S(1)}, u32[]{:S(2)}, u32[]{:S(2)}) collective-permute-start(f32[2,128,128]{2,1,0:T(8,128)S(1)} %copy-done.1), channel_id=1, source_target_pairs={{1,0},{2,1},{3,2},{4,3},{5,4},{6,5},{7,6},{8,7},{9,8},{10,9},{11,1... | collective-permute-start | bytes 393224 | tf_op jit(solution)/shard_map/ppermute | solution.py:22
  33.4 7.6 %collective-permute-done.3 = f32[2,128,128]{2,1,0:T(8,128)S(1)} collective-permute-done((f32[2,128,128]{2,1,0:T(8,128)S(1)}, f32[2,128,128]{2,1,0:T(8,128)S(1)}, u32[]{:S(2)}, u32[]{:S(2)}) %collective-permute-start.3) | collective-permute-done | bytes 131104 | tf_op jit(solution)/shard_map/ppermute | solution.py:22
  41.0 1.4 %fusion.33 = (f32[6,128,128]{2,1,0:T(8,128)S(1)}, f32[6,128,128]{2,1,0:T(8,128)S(1)}, f32[6,128,128]{2,1,0:T(8,128)S(1)}, f32[6,128,128]{2,1,0:T(8,128)S(1)}) fusion(f32[6,128,128]{2,1,0:T(8,128)S(1)} %constant_dynamic-update-slice_fusion, f32[]{:T(128)} %bitcast, f32[]{:T(128)} %bitcast.1), kind=kLoop, calls=%fused_computation.110 | loop fusion | flops 884736 | bytes 1966088 | tf_op jit(solution)/shard_map/neg | solution.py:78
  46.5 1.9 %collective-permute-start.6 = (f32[2,2,2,128,128]{4,3,2,1,0:T(8,128)S(1)}, f32[2,2,2,128,128]{4,3,2,1,0:T(8,128)S(1)}, u32[]{:S(2)}, u32[]{:S(2)}) collective-permute-start(f32[2,2,2,128,128]{4,3,2,1,0:T(8,128)S(1)} %slice_add_fusion.13), channel_id=1, source_target_pairs={{0,1},{1,2},{2,3},{3,4},{4,5},{5,6},{6,7},{7,8},{8,9},{9,10},{10,1... | collective-permute-start | bytes 1572872 | tf_op jit(solution)/shard_map/ppermute | solution.py:20
  48.5 2.4 %collective-permute-start.7 = (f32[2,2,2,128,128]{4,3,2,1,0:T(8,128)S(1)}, f32[2,2,2,128,128]{4,3,2,1,0:T(8,128)S(1)}, u32[]{:S(2)}, u32[]{:S(2)}) collective-permute-start(f32[2,2,2,128,128]{4,3,2,1,0:T(8,128)S(1)} %slice_add_fusion.13), channel_id=1, source_target_pairs={{1,0},{2,1},{3,2},{4,3},{5,4},{6,5},{7,6},{8,7},{9,8},{10,9},{11,1... | collective-permute-start | bytes 1572872 | tf_op jit(solution)/shard_map/ppermute | solution.py:22
  50.9 3.7 %collective-permute-done.6 = f32[2,2,2,128,128]{4,3,2,1,0:T(8,128)S(1)} collective-permute-done((f32[2,2,2,128,128]{4,3,2,1,0:T(8,128)S(1)}, f32[2,2,2,128,128]{4,3,2,1,0:T(8,128)S(1)}, u32[]{:S(2)}, u32[]{:S(2)}) %collective-permute-start.6) | collective-permute-done | bytes 524320 | tf_op jit(solution)/shard_map/ppermute | solution.py:20
  54.6 7.7 %collective-permute-done.7 = f32[2,2,2,128,128]{4,3,2,1,0:T(8,128)S(1)} collective-permute-done((f32[2,2,2,128,128]{4,3,2,1,0:T(8,128)S(1)}, f32[2,2,2,128,128]{4,3,2,1,0:T(8,128)S(1)}, u32[]{:S(2)}, u32[]{:S(2)}) %collective-permute-start.7) | collective-permute-done | bytes 524320 | tf_op jit(solution)/shard_map/ppermute | solution.py:22
  65.5 1.9 %collective-permute-start.8 = (f32[2,2,2,128,128]{4,3,2,1,0:T(8,128)S(1)}, f32[2,2,2,128,128]{4,3,2,1,0:T(8,128)S(1)}, u32[]{:S(2)}, u32[]{:S(2)}) collective-permute-start(f32[2,2,2,128,128]{4,3,2,1,0:T(8,128)S(1)} %fusion.24), channel_id=1, source_target_pairs={{0,1},{1,2},{2,3},{3,4},{4,5},{5,6},{6,7},{7,8},{8,9},{9,10},{10,1... | collective-permute-start | bytes 1572872 | tf_op jit(solution)/shard_map/ppermute | solution.py:20
  67.4 2.4 %collective-permute-start.9 = (f32[2,2,2,128,128]{4,3,2,1,0:T(8,128)S(1)}, f32[2,2,2,128,128]{4,3,2,1,0:T(8,128)S(1)}, u32[]{:S(2)}, u32[]{:S(2)}) collective-permute-start(f32[2,2,2,128,128]{4,3,2,1,0:T(8,128)S(1)} %fusion.24), channel_id=1, source_target_pairs={{1,0},{2,1},{3,2},{4,3},{5,4},{6,5},{7,6},{8,7},{9,8},{10,9},{11,1... | collective-permute-start | bytes 1572872 | tf_op jit(solution)/shard_map/ppermute | solution.py:22
  69.9 3.6 %collective-permute-done.8 = f32[2,2,2,128,128]{4,3,2,1,0:T(8,128)S(1)} collective-permute-done((f32[2,2,2,128,128]{4,3,2,1,0:T(8,128)S(1)}, f32[2,2,2,128,128]{4,3,2,1,0:T(8,128)S(1)}, u32[]{:S(2)}, u32[]{:S(2)}) %collective-permute-start.8) | collective-permute-done | bytes 524320 | tf_op jit(solution)/shard_map/ppermute | solution.py:20
  73.5 7.7 %collective-permute-done.9 = f32[2,2,2,128,128]{4,3,2,1,0:T(8,128)S(1)} collective-permute-done((f32[2,2,2,128,128]{4,3,2,1,0:T(8,128)S(1)}, f32[2,2,2,128,128]{4,3,2,1,0:T(8,128)S(1)}, u32[]{:S(2)}, u32[]{:S(2)}) %collective-permute-start.9) | collective-permute-done | bytes 524320 | tf_op jit(solution)/shard_map/ppermute | solution.py:22
  83.0 1.9 %collective-permute-start.10 = (f32[2,2,2,128,128]{4,3,2,1,0:T(8,128)S(1)}, f32[2,2,2,128,128]{4,3,2,1,0:T(8,128)S(1)}, u32[]{:S(2)}, u32[]{:S(2)}) collective-permute-start(f32[2,2,2,128,128]{4,3,2,1,0:T(8,128)S(1)} %slice_add_fusion.7), channel_id=1, source_target_pairs={{0,1},{1,2},{2,3},{3,4},{4,5},{5,6},{6,7},{7,8},{8,9},{9,10},{10,1... | collective-permute-start | bytes 1572872 | tf_op jit(solution)/shard_map/ppermute | solution.py:20
  84.9 2.6 %collective-permute-start.11 = (f32[2,2,2,128,128]{4,3,2,1,0:T(8,128)S(1)}, f32[2,2,2,128,128]{4,3,2,1,0:T(8,128)S(1)}, u32[]{:S(2)}, u32[]{:S(2)}) collective-permute-start(f32[2,2,2,128,128]{4,3,2,1,0:T(8,128)S(1)} %slice_add_fusion.7), channel_id=1, source_target_pairs={{1,0},{2,1},{3,2},{4,3},{5,4},{6,5},{7,6},{8,7},{9,8},{10,9},{11,1... | collective-permute-start | bytes 1572872 | tf_op jit(solution)/shard_map/ppermute | solution.py:22
  87.5 3.5 %collective-permute-done.10 = f32[2,2,2,128,128]{4,3,2,1,0:T(8,128)S(1)} collective-permute-done((f32[2,2,2,128,128]{4,3,2,1,0:T(8,128)S(1)}, f32[2,2,2,128,128]{4,3,2,1,0:T(8,128)S(1)}, u32[]{:S(2)}, u32[]{:S(2)}) %collective-permute-start.10) | collective-permute-done | bytes 524320 | tf_op jit(solution)/shard_map/ppermute | solution.py:20
  91.0 7.7 %collective-permute-done.11 = f32[2,2,2,128,128]{4,3,2,1,0:T(8,128)S(1)} collective-permute-done((f32[2,2,2,128,128]{4,3,2,1,0:T(8,128)S(1)}, f32[2,2,2,128,128]{4,3,2,1,0:T(8,128)S(1)}, u32[]{:S(2)}, u32[]{:S(2)}) %collective-permute-start.11) | collective-permute-done | bytes 524320 | tf_op jit(solution)/shard_map/ppermute | solution.py:22
  102.0 27.3 %all_to_all.5 = f32[8,2,2,16,128]{4,3,2,1,0:T(8,128)S(1)} all-to-all(f32[8,2,2,16,128]{4,3,2,1,0:T(8,128)S(1)} %copy.8), channel_id=1, replica_groups=mesh['freq'=8,'space'=64] {'freq'}, dimensions={0} | all-to-all | bytes 524288 | tf_op jit(solution)/shard_map/all_to_all | solution.py:36
  (84 shorter events, 15.6 us)
Async XLA Ops:
  0.0 21.6 %copy-start.1 = (f32[2,128,128]{2,1,0:T(8,128)S(1)}, f32[2,128,128]{2,1,0:T(8,128)}, u32[]{:S(2)}) copy-start(f32[2,128,128]{2,1,0:T(8,128)} %param.7) | copy-start | bytes 393220
  0.0 42.6 %collective-permute-start = (f32[2,2,2,128,128]{4,3,2,1,0:T(8,128)S(1)}, f32[2,2,2,128,128]{4,3,2,1,0:T(8,128)S(1)}, u32[]{:S(2)}, u32[]{:S(2)}) collective-permute-start(f32[2,2,2,128,128]{4,3,2,1,0:T(8,128)S(1)} %broadcast.193), channel_id=1, source_target_pairs={{0,1},{1,2},{2,3},{3,4},{4,5},{5,6},{6,7},{7,8},{8,9},{9,10},{10,1... | collective-permute-start | bytes 1572872 | tf_op jit(solution)/shard_map/ppermute | solution.py:20
  5.4 37.3 %collective-permute-start.1 = (f32[2,2,2,128,128]{4,3,2,1,0:T(8,128)S(1)}, f32[2,2,2,128,128]{4,3,2,1,0:T(8,128)S(1)}, u32[]{:S(2)}, u32[]{:S(2)}) collective-permute-start(f32[2,2,2,128,128]{4,3,2,1,0:T(8,128)S(1)} %broadcast.193), channel_id=1, source_target_pairs={{1,0},{2,1},{3,2},{4,3},{5,4},{6,5},{7,6},{8,7},{9,8},{10,9},{11,1... | collective-permute-start | bytes 1572872 | tf_op jit(solution)/shard_map/ppermute | solution.py:22
  12.8 31.4 %collective-permute-start.4 = (f32[2,2,2,128,128]{4,3,2,1,0:T(8,128)}, f32[2,2,2,128,128]{4,3,2,1,0:T(8,128)S(1)}, u32[]{:S(2)}, u32[]{:S(2)}) collective-permute-start(f32[2,2,2,128,128]{4,3,2,1,0:T(8,128)} %pad_maximum_fusion.10), channel_id=1, source_target_pairs={{0,1},{1,2},{2,3},{3,4},{4,5},{5,6},{6,7},{7,8},{8,9},{9,10},{10,1... | collective-permute-start | bytes 1572872 | tf_op jit(solution)/shard_map/ppermute | solution.py:20
  19.7 24.4 %collective-permute-start.5 = (f32[2,2,2,128,128]{4,3,2,1,0:T(8,128)}, f32[2,2,2,128,128]{4,3,2,1,0:T(8,128)S(1)}, u32[]{:S(2)}, u32[]{:S(2)}) collective-permute-start(f32[2,2,2,128,128]{4,3,2,1,0:T(8,128)} %pad_maximum_fusion.10), channel_id=1, source_target_pairs={{1,0},{2,1},{3,2},{4,3},{5,4},{6,5},{7,6},{8,7},{9,8},{10,9},{11,1... | collective-permute-start | bytes 1572872 | tf_op jit(solution)/shard_map/ppermute | solution.py:22
  21.7 8.9 %collective-permute-start.2 = (f32[2,128,128]{2,1,0:T(8,128)S(1)}, f32[2,128,128]{2,1,0:T(8,128)}, u32[]{:S(2)}, u32[]{:S(2)}) collective-permute-start(f32[2,128,128]{2,1,0:T(8,128)S(1)} %copy-done.1), channel_id=1, source_target_pairs={{0,1},{1,2},{2,3},{3,4},{4,5},{5,6},{6,7},{7,8},{8,9},{9,10},{10,1... | collective-permute-start | bytes 393224 | tf_op jit(solution)/shard_map/ppermute | solution.py:20
  30.6 10.4 %collective-permute-start.3 = (f32[2,128,128]{2,1,0:T(8,128)S(1)}, f32[2,128,128]{2,1,0:T(8,128)S(1)}, u32[]{:S(2)}, u32[]{:S(2)}) collective-permute-start(f32[2,128,128]{2,1,0:T(8,128)S(1)} %copy-done.1), channel_id=1, source_target_pairs={{1,0},{2,1},{3,2},{4,3},{5,4},{6,5},{7,6},{8,7},{9,8},{10,9},{11,1... | collective-permute-start | bytes 393224 | tf_op jit(solution)/shard_map/ppermute | solution.py:22
  45.3 1.0 copy-start
  46.4 4.5 %copy-start.2 = (s32[2,128,128]{2,1,0:T(8,128)S(1)}, s32[2,128,128]{2,1,0:T(8,128)}, u32[]{:S(2)}) copy-start(s32[2,128,128]{2,1,0:T(8,128)} %param.9) | copy-start | bytes 393220
  46.5 8.0 %collective-permute-start.6 = (f32[2,2,2,128,128]{4,3,2,1,0:T(8,128)S(1)}, f32[2,2,2,128,128]{4,3,2,1,0:T(8,128)S(1)}, u32[]{:S(2)}, u32[]{:S(2)}) collective-permute-start(f32[2,2,2,128,128]{4,3,2,1,0:T(8,128)S(1)} %slice_add_fusion.13), channel_id=1, source_target_pairs={{0,1},{1,2},{2,3},{3,4},{4,5},{5,6},{6,7},{7,8},{8,9},{9,10},{10,1... | collective-permute-start | bytes 1572872 | tf_op jit(solution)/shard_map/ppermute | solution.py:20
  48.5 13.8 %collective-permute-start.7 = (f32[2,2,2,128,128]{4,3,2,1,0:T(8,128)S(1)}, f32[2,2,2,128,128]{4,3,2,1,0:T(8,128)S(1)}, u32[]{:S(2)}, u32[]{:S(2)}) collective-permute-start(f32[2,2,2,128,128]{4,3,2,1,0:T(8,128)S(1)} %slice_add_fusion.13), channel_id=1, source_target_pairs={{1,0},{2,1},{3,2},{4,3},{5,4},{6,5},{7,6},{8,7},{9,8},{10,9},{11,1... | collective-permute-start | bytes 1572872 | tf_op jit(solution)/shard_map/ppermute | solution.py:22
  65.5 8.0 %collective-permute-start.8 = (f32[2,2,2,128,128]{4,3,2,1,0:T(8,128)S(1)}, f32[2,2,2,128,128]{4,3,2,1,0:T(8,128)S(1)}, u32[]{:S(2)}, u32[]{:S(2)}) collective-permute-start(f32[2,2,2,128,128]{4,3,2,1,0:T(8,128)S(1)} %fusion.24), channel_id=1, source_target_pairs={{0,1},{1,2},{2,3},{3,4},{4,5},{5,6},{6,7},{7,8},{8,9},{9,10},{10,1... | collective-permute-start | bytes 1572872 | tf_op jit(solution)/shard_map/ppermute | solution.py:20
  67.4 13.8 %collective-permute-start.9 = (f32[2,2,2,128,128]{4,3,2,1,0:T(8,128)S(1)}, f32[2,2,2,128,128]{4,3,2,1,0:T(8,128)S(1)}, u32[]{:S(2)}, u32[]{:S(2)}) collective-permute-start(f32[2,2,2,128,128]{4,3,2,1,0:T(8,128)S(1)} %fusion.24), channel_id=1, source_target_pairs={{1,0},{2,1},{3,2},{4,3},{5,4},{6,5},{7,6},{8,7},{9,8},{10,9},{11,1... | collective-permute-start | bytes 1572872 | tf_op jit(solution)/shard_map/ppermute | solution.py:22
  83.0 8.0 %collective-permute-start.10 = (f32[2,2,2,128,128]{4,3,2,1,0:T(8,128)S(1)}, f32[2,2,2,128,128]{4,3,2,1,0:T(8,128)S(1)}, u32[]{:S(2)}, u32[]{:S(2)}) collective-permute-start(f32[2,2,2,128,128]{4,3,2,1,0:T(8,128)S(1)} %slice_add_fusion.7), channel_id=1, source_target_pairs={{0,1},{1,2},{2,3},{3,4},{4,5},{5,6},{6,7},{7,8},{8,9},{9,10},{10,1... | collective-permute-start | bytes 1572872 | tf_op jit(solution)/shard_map/ppermute | solution.py:20
  84.9 13.8 %collective-permute-start.11 = (f32[2,2,2,128,128]{4,3,2,1,0:T(8,128)S(1)}, f32[2,2,2,128,128]{4,3,2,1,0:T(8,128)S(1)}, u32[]{:S(2)}, u32[]{:S(2)}) collective-permute-start(f32[2,2,2,128,128]{4,3,2,1,0:T(8,128)S(1)} %slice_add_fusion.7), channel_id=1, source_target_pairs={{1,0},{2,1},{3,2},{4,3},{5,4},{6,5},{7,6},{8,7},{9,8},{10,9},{11,1... | collective-permute-start | bytes 1572872 | tf_op jit(solution)/shard_map/ppermute | solution.py:22
where the time goes:
time: 131 us; the launch traced here: 130 us
  waiting for transfers between devices  43.3 us (33%)
  starting transfers between devices  38.2 us (29%)
  blocking collectives  27.3 us (21%)
  other arithmetic  14.7 us (11%)
  local copies, waits for them, and re-layouts  5.89 us (4%)
    ppermute x6, waiting for transfers between devices, padded(): lax.ppermute(head, axis, [((i + 1) % count, i) for i in range(ends)])  30.7 us
    all_to_all x1, blocking collectives, summed_on_arrival(): lax.all_to_all(parts, axis, split_axis=0, concat_axis=0, tiled=True)  27.3 us
    ppermute x6, starting transfers between devices, padded(): lax.ppermute(tail, axis, [(i, (i + 1) % count) for i in range(ends)])  25 us
    ppermute x6, starting transfers between devices, padded(): lax.ppermute(head, axis, [((i + 1) % count, i) for i in range(ends)])  13.1 us
    ppermute x6, waiting for transfers between devices, padded(): lax.ppermute(tail, axis, [(i, (i + 1) % count) for i in range(ends)])  12.6 us
    add x7, other arithmetic, neighbours(): beside_all + jnp.pad(center[:, :, :, :, 1:], pad_z_low)  3.57 us
  transfers between devices with their start and end apart: 12, of which 8 were waited for; matrix products, arithmetic and copies ran while one was open for 7% of the time, Pallas kernels for 0%

commit v1 on v0

v1 whole, which is shorter than its diff:
```python
import functools

import jax
import jax.numpy as jnp
from jax import lax
from jax.experimental import pallas as pl
from jax.experimental.pallas import tpu as pltpu
from jax.sharding import PartitionSpec as P


OMEGA = 0.8
KEEP = 1.0 - OMEGA
TOP = 8
ROWS = 32


def multiply(x, y):
    return (x[0] * y[0] - x[1] * y[1], x[0] * y[1] + x[1] * y[0])


def multiply_conj(x, y):
    return (x[0] * y[0] + x[1] * y[1], x[0] * y[1] - x[1] * y[0])


def inverse(medium, shift_re, shift_im):
    diag_re = 6.0 + shift_re * medium
    diag_im = shift_im * medium
    scale = OMEGA / (diag_re * diag_re + diag_im * diag_im)
    return (diag_re * scale, -diag_im * scale)


def chunks(height):
    return [(r, min(ROWS, height - r)) for r in range(0, height, ROWS)]


def clear_edges(pad):
    height = pad.shape[-2] - 2 * TOP
    zero = jnp.zeros((TOP, pad.shape[-1]), jnp.float32)
    for part in range(pad.shape[0]):
        pad[part, 0:TOP] = zero
        pad[part, TOP + height :] = zero


def in_plane(pad, part, r, n):
    here = pad[part, TOP + r : TOP + r + n]
    width = here.shape[-1]
    lane = lax.broadcasted_iota(jnp.int32, here.shape, 1)
    left = jnp.where(lane == 0, 0.0, pltpu.roll(here, 1, 1))
    right = jnp.where(lane == width - 1, 0.0, pltpu.roll(here, width - 1, 1))
    above = pad[part, TOP + r - 1 : TOP + r - 1 + n]
    below = pad[part, TOP + r + 1 : TOP + r + 1 + n]
    return here, (left + right) + (above + below)


def complex_in_plane(pad, layer, r, n):
    re, sum_re = in_plane(pad, 2 * layer, r, n)
    im, sum_im = in_plane(pad, 2 * layer + 1, r, n)
    return (re, im), (sum_re, sum_im)


def store(ref, at, r, n, value):
    ref[at, r : r + n] = value[0]
    ref[at + 1, r : r + n] = value[1]


def load(ref, at, r, n):
    return (ref[at, r : r + n], ref[at + 1, r : r + n])


def add(x, y):
    return (x[0] + y[0], x[1] + y[1])


def scale(a, x):
    return (a * x[0], a * x[1])


def side():
    return lax.rem(lax.axis_index("space"), 2)


def has_partner():
    at = lax.axis_index("space")
    last = lax.axis_size("space") - 1
    return jnp.where((at == 0) | (at == last), 0.0, 1.0).astype(jnp.float32)


def start_kernel(
    shifts_hbm, back_hbm, probes_hbm, medium_hbm, receivers_hbm,
    out_a0, out_a1, out_b, inv, waves, row,
    shifts, back, probes, medium, receivers, pad, sems,
):
    copies = [
        pltpu.make_async_copy(src, dst, sems.at[k])
        for k, (src, dst) in enumerate(
            (
                (shifts_hbm, shifts),
                (medium_hbm, medium),
                (back_hbm, back),
                (probes_hbm, probes),
                (receivers_hbm, receivers),
            )
        )
    ]
    for copy in copies:
        copy.start()
    near = side()
    own = (near, 1 - near)
    height = medium.shape[1]
    outs = ((out_a0, 0), (out_a1, 0)), ((out_b, 0), (out_b, 5))
    clear_edges(pad)
    copies[0].wait()
    shift_re, shift_im = shifts[0, 0], shifts[0, 1]
    row[0] = jnp.full(row.shape[1:], shift_re, jnp.float32)
    row[1] = jnp.full(row.shape[1:], shift_im, jnp.float32)
    copies[1].wait()
    for layer in range(2):
        for r, n in chunks(height):
            med = medium[own[layer], r : r + n]
            store(inv, 2 * layer, r, n, inverse(med, shift_re, shift_im))
            outs[layer][0][0][outs[layer][0][1] + 4, r : r + n] = med
    copies[2].wait()
    for layer in range(2):
        for r, n in chunks(height):
            rows = slice(r, r + n)
            bg = (back[0, 0, own[layer], rows], back[0, 1, own[layer], rows])
            store(waves, 2 * layer, r, n, multiply((shift_re, shift_im), bg))
    copies[3].wait()
    for p in range(2):
        for layer in range(2):
            ref, at = outs[layer][p]
            for r, n in chunks(height):
                probe = probes[p, own[layer], r : r + n]
                first = scale(probe, multiply(load(inv, 2 * layer, r, n), load(waves, 2 * layer, r, n)))
                store(ref, at, r, n, first)
                store(pad, 2 * layer, TOP + r, n, first)
        for layer in range(2):
            ref, at = outs[layer][p]
            for r, n in chunks(height):
                here, around = complex_in_plane(pad, layer, r, n)
                around = add(around, load(pad, 2 * (1 - layer), TOP + r, n))
                part = add(scale(1.0 + KEEP, here), multiply(load(inv, 2 * layer, r, n), around))
                store(ref, at + 2, r, n, part)
    copies[4].wait()
    for layer in range(2):
        ref, at = outs[layer][1]
        for r, n in chunks(height):
            ref[at + 4, r : r + n] = receivers[own[layer], r : r + n].astype(jnp.float32)


def halo_inverse(med, layer, row, mask):
    re, im = inverse(med, row[0, 0:1], row[1, 0:1])
    return (mask * re, mask * im) if layer == 0 else (re, im)


def forward_kernel(p, row, own_a, own_b, got_a, got_b, med_a, inv, *rest):
    if p == 0:
        out_a, out_b, pad, spare = rest
        b_at, out_at = 0, 0
    else:
        first_b, out_a, out_b, pad, spare = rest
        b_at, out_at = 5, 4
        out_b[0:4] = first_b[...]
    mask = has_partner()
    height = inv.shape[1]
    own = ((own_a, 0), (own_b, b_at))
    got = ((got_a, 0), (got_b, b_at))
    med = ((med_a, 4), (got_b, 4))
    out = ((out_a, 0), (out_b, out_at))
    clear_edges(pad)
    clear_edges(spare)
    for layer in range(2):
        (mine, at), (theirs, from_) = own[layer], got[layer]
        for r, n in chunks(height):
            second = add(
                load(mine, at + 2, r, n),
                multiply(load(inv, 2 * layer, r, n), load(theirs, from_, r, n)),
            )
            store(pad, 2 * layer, TOP + r, n, second)
    for layer in range(2):
        (mine, at), (theirs, from_) = own[layer], got[layer]
        for r, n in chunks(height):
            first = load(mine, at, r, n)
            there = halo_inverse(med[layer][0][med[layer][1], r : r + n], layer, row, mask)
            halo = add(load(theirs, from_ + 2, r, n), multiply(there, first))
            here, around = complex_in_plane(pad, layer, r, n)
            around = add(add(around, halo), load(pad, 2 * (1 - layer), TOP + r, n))
            third = add(
                add(scale(KEEP, here), first), multiply(load(inv, 2 * layer, r, n), around)
            )
            store(spare, 2 * layer, TOP + r, n, third)
            store(out[layer][0], out[layer][1], r, n, third)
    for layer in range(2):
        mine, at = own[layer]
        for r, n in chunks(height):
            here, around = complex_in_plane(spare, layer, r, n)
            around = add(around, load(spare, 2 * (1 - layer), TOP + r, n))
            part = add(
                add(scale(KEEP, here), load(mine, at, r, n)),
                multiply(load(inv, 2 * layer, r, n), around),
            )
            store(out[layer][0], out[layer][1] + 2, r, n, part)


def turn_kernel(
    p, row, own_a, own_b, got_a, got_b, med_a, got_b1, rec_a, own_a1, own_b1, inv, *rest
):
    if p == 0:
        out_a, out_b, right, pad, spare = rest
        b_at, out_at = 0, 0
    else:
        first_b, out_a, out_b, right, pad, spare = rest
        b_at, out_at = 4, 4
        out_b[0:4] = first_b[...]
    mask = has_partner()
    height = inv.shape[1]
    own = ((own_a, 0), (own_b, 0 if p == 0 else b_at))
    got = ((got_a, 0), (got_b, b_at))
    med = ((med_a, 4), (got_b1, 4))
    rec_own = ((own_a1, 4), (own_b1, 9))
    rec_got = ((rec_a, 4), (got_b1, 9))
    out = ((out_a, 0), (out_b, out_at))
    clear_edges(pad)
    clear_edges(spare)
    for layer in range(2):
        (mine, at), (theirs, from_) = own[layer], got[layer]
        for r, n in chunks(height):
            there = load(inv, 2 * layer, r, n)
            fourth = add(load(mine, at + 2, r, n), multiply(there, load(theirs, from_, r, n)))
            heard = scale(rec_own[layer][0][rec_own[layer][1], r : r + n], fourth)
            first = multiply_conj(there, heard)
            store(pad, 2 * layer, TOP + r, n, first)
            store(right, 2 * layer, r, n, first)
    for layer in range(2):
        (mine, at), (theirs, from_) = own[layer], got[layer]
        for r, n in chunks(height):
            there = halo_inverse(med[layer][0][med[layer][1], r : r + n], layer, row, mask)
            fourth = add(load(theirs, from_ + 2, r, n), multiply(there, load(mine, at, r, n)))
            halo = multiply_conj(
                there, scale(rec_got[layer][0][rec_got[layer][1], r : r + n], fourth)
            )
            here, around = complex_in_plane(pad, layer, r, n)
            around = add(add(around, halo), load(pad, 2 * (1 - layer), TOP + r, n))
            second = add(
                scale(1.0 + KEEP, here), multiply_conj(load(inv, 2 * layer, r, n), around)
            )
            store(spare, 2 * layer, TOP + r, n, second)
            store(out[layer][0], out[layer][1], r, n, second)
    for layer in range(2):
        for r, n in chunks(height):
            here, around = complex_in_plane(spare, layer, r, n)
            around = add(around, load(spare, 2 * (1 - layer), TOP + r, n))
            part = add(
                add(scale(KEEP, here), load(right, 2 * layer, r, n)),
                multiply_conj(load(inv, 2 * layer, r, n), around),
            )
            store(out[layer][0], out[layer][1] + 2, r, n, part)


def end_kernel(p, row, own_a, own_b, got_a, got_b, med_a, got_b1, inv, right, waves, *rest):
    if p == 0:
        out, pad = rest
        b_at, out_at = 0, 0
    else:
        first_out, out, pad = rest
        b_at, out_at = 4, 1
        out[:, 0:1] = first_out[...]
    mask = has_partner()
    near = side()
    place = (near, 1 - near)
    height = inv.shape[1]
    strip = out.shape[3]
    own = ((own_a, 0), (own_b, 0 if p == 0 else b_at))
    got = ((got_a, 0), (got_b, b_at))
    med = ((med_a, 4), (got_b1, 4))
    clear_edges(pad)
    for layer in range(2):
        (mine, at), (theirs, from_) = own[layer], got[layer]
        for r, n in chunks(height):
            third = add(
                load(mine, at + 2, r, n),
                multiply_conj(load(inv, 2 * layer, r, n), load(theirs, from_, r, n)),
            )
            store(pad, 2 * layer, TOP + r, n, third)
    for layer in range(2):
        (mine, at), (theirs, from_) = own[layer], got[layer]
        for r, n in chunks(height):
            there = halo_inverse(med[layer][0][med[layer][1], r : r + n], layer, row, mask)
            halo = add(
                load(theirs, from_ + 2, r, n), multiply_conj(there, load(mine, at, r, n))
            )
            here, around = complex_in_plane(pad, layer, r, n)
            around = add(add(around, halo), load(pad, 2 * (1 - layer), TOP + r, n))
            fourth = add(
                add(scale(KEEP, here), load(right, 2 * layer, r, n)),
                multiply_conj(load(inv, 2 * layer, r, n), around),
            )
            wave = load(waves, 2 * layer, r, n)
            term = wave[0] * fourth[0] + wave[1] * fourth[1]
            for k in range(0, n, strip):
                out[(r + k) // strip, out_at, place[layer]] = term[k : k + strip]


def call(kernel, shapes, scratch, *args, space=pltpu.VMEM):
    vmem = pl.BlockSpec(memory_space=pltpu.VMEM)
    return pl.pallas_call(
        kernel,
        out_shape=[jax.ShapeDtypeStruct(s, jnp.float32) for s in shapes],
        in_specs=[pl.BlockSpec(memory_space=space)] * len(args),
        out_specs=[vmem] * len(shapes),
        scratch_shapes=scratch,
        cost_estimate=pl.CostEstimate(flops=2_000_000, bytes_accessed=2_000_000, transcendentals=0),
        compiler_params=pltpu.CompilerParams(vmem_limit_bytes=16 * 1024 * 1024),
    )(*args)


def swap_links(x):
    count = lax.axis_size("space")
    pairs = []
    for i in range(1, count - 1, 2):
        pairs += [(i, i + 1), (i + 1, i)]
    return lax.ppermute(x, "space", pairs)


def swap_cores(x):
    pairs = []
    for i in range(0, lax.axis_size("space"), 2):
        pairs += [(i, i + 1), (i + 1, i)]
    return lax.ppermute(x, "space", pairs)


def per_device(probes, background, medium, shifts, receivers):
    plane = medium.shape[1:]
    pad = pltpu.VMEM((4, plane[0] + 2 * TOP, plane[1]), jnp.float32)
    five, ten, four, eight = [(k, *plane) for k in (5, 10, 4, 8)]
    args = (shifts, background, probes, medium, receivers)
    held = [pltpu.VMEM(v.shape, v.dtype) for v in args[1:]]
    a1 = [None, None]
    a1[0], a1[1], b1, inv, waves, row = call(
        start_kernel,
        [five, five, ten, four, four, (2, 8, plane[1])],
        [pltpu.SMEM(shifts.shape, shifts.dtype), *held, pad, pltpu.SemaphoreType.DMA((5,))],
        *args,
        space=pltpu.HBM,
    )
    ra1 = [swap_links(a1[p]) for p in range(2)]
    rb1 = swap_cores(b1)
    a2, ra2, b2 = [None, None], [None, None], []
    for p in range(2):
        a2[p], out_b = call(
            functools.partial(forward_kernel, p),
            [four, eight if p else four],
            [pad, pad],
            row, a1[p], b1, ra1[p], rb1, ra1[0], inv, *b2,
        )
        b2.append(out_b)
        ra2[p] = swap_links(a2[p])
    rb2 = swap_cores(b2[1])
    a3, ra3, b3, right = [None, None], [None, None], [], [None, None]
    for p in range(2):
        a3[p], out_b, right[p] = call(
            functools.partial(turn_kernel, p),
            [four, eight if p else four, four],
            [pad, pad],
            row, a2[p], b2[p], ra2[p], rb2, ra1[0], rb1, ra1[1], a1[1], b1, inv, *b3,
        )
        b3.append(out_b)
        ra3[p] = swap_links(a3[p])
    rb3 = swap_cores(b3[1])
    blocks = lax.axis_size("freq")
    terms = []
    for p in range(2):
        (out,) = call(
            functools.partial(end_kernel, p),
            [(blocks, p + 1, 2, plane[0] // blocks, plane[1])],
            [pad],
            row, a3[p], b3[p], ra3[p], rb3, ra1[0], rb1, inv, right[p], waves, *terms,
        )
        terms.append(out)
    arrived = lax.all_to_all(terms[1], "freq", split_axis=0, concat_axis=0, tiled=True)
    return arrived.sum(axis=0)


def solution(mesh):
    in_specs = (
        P(None, "space", None, None),
        P("freq", None, "space", None, None),
        P("space", None, None),
        P("freq", None),
        P("space", None, None),
    )
    out_specs = P(None, "space", "freq", None)
    return jax.shard_map(
        per_device, mesh=mesh, in_specs=in_specs, out_specs=out_specs, check_vma=False
    )
```

time: 131 us -> 95.2 us (0.73)
  the two profiles are of different devices: /device:TPU:103 before, /device:TPU:32 now
where the time goes in v1:
time: 95.2 us; the launch traced here: 94.7 us
  blocking collectives  39.4 us (41%)
  starting transfers between devices  28.8 us (30%)
  waiting for transfers between devices  17.8 us (19%)
  local copies, waits for them, and re-layouts  4.36 us (5%)
  Pallas kernels  3.63 us (4%)
    all_to_all x1, blocking collectives, per_device(): lax.all_to_all(terms[1], 'freq', split_axis=0, concat_axis=0, tiled=True)  39.4 us
    ppermute x6, starting transfers between devices, swap_links(): return lax.ppermute(x, 'space', pairs)  23 us
    ppermute x6, waiting for transfers between devices, swap_links(): return lax.ppermute(x, 'space', pairs)  17.8 us
    ppermute x3, starting transfers between devices, swap_cores(): return lax.ppermute(x, 'space', pairs)  5.76 us
    unnamed x10, local copies, waits for them, and re-layouts  4.36 us
    pallas_call x7, Pallas kernels, call(): pl.pallas_call(kernel, out_shape=[jax.ShapeDtypeStruct(s, jnp.float32) fo...  3.63 us
  transfers between devices with their start and end apart: 9, of which 6 were waited for; matrix products, arithmetic and copies ran while one was open for 0% of the time, Pallas kernels for 1%

profile of v1, /device:TPU:32, one launch (start us, length us, event | category | flops | bytes accessed | tf_op | source)
XLA Modules:
  0.0 94.7 jit_solution(18188160781565185405)
XLA Ops:
  0.0 0.9 %copy-done = f32[1,2,2,128,128]{4,3,2,1,0:T(8,128)S(1)} copy-done((f32[1,2,2,128,128]{4,3,2,1,0:T(8,128)S(1)}, f32[1,2,2,128,128]{4,3,2,1,0:T(8,128)}, u32[]{:S(2)}) %copy-start) | copy-done | bytes 262168
  1.0 0.9 %copy-done.1 = f32[2,2,128,128]{3,2,1,0:T(8,128)S(1)} copy-done((f32[2,2,128,128]{3,2,1,0:T(8,128)S(1)}, f32[2,2,128,128]{3,2,1,0:T(8,128)}, u32[]{:S(2)}) %copy-start.1) | copy-done | bytes 262168
  1.9 0.9 copy-done.2
  2.8 0.9 copy-done.3
  3.7 0.7 copy-done.4
  4.4 1.1 %shard_map.55 = (f32[5,128,128]{2,1,0:T(8,128)S(1)}, f32[5,128,128]{2,1,0:T(8,128)S(1)}, f32[10,128,128]{2,1,0:T(8,128)S(1)}, f32[4,128,128]{2,1,0:T(8,128)S(1)}...) custom-call(f32[1,2]{1,0:T(1,128)S(1)} %copy-done.4, f32[1,2,2,128,128]{4,3,2,1,0:T(8,128)S(1)} %copy-done, ...), custom_call_target="tpu_custom_call" | custom-call | flops 2000000 | bytes 2000000 | tf_op jit(solution)/shard_map/pallas_call | solution.py:306
  5.5 1.9 %collective-permute-start.1 = (f32[10,128,128]{2,1,0:T(8,128)S(1)}, f32[10,128,128]{2,1,0:T(8,128)S(1)}, u32[]{:S(2)}, u32[]{:S(2)}) collective-permute-start(f32[10,128,128]{2,1,0:T(8,128)S(1)} %get-tuple-element.23.own_b.own_b1), channel_id=1, source_target_pairs={{0,1},{1,0},{2,3},{3,2},{4,5},{5,4},{6,7},{7,6},{8,9},{9,8},{10,11... | collective-permute-start | bytes 1966088 | tf_op jit(solution)/shard_map/ppermute | solution.py:329
  7.4 4.3 %collective-permute-start.2 = (f32[5,128,128]{2,1,0:T(8,128)S(1)}, f32[5,128,128]{2,1,0:T(8,128)S(1)}, u32[]{:S(2)}, u32[]{:S(2)}) collective-permute-start(f32[5,128,128]{2,1,0:T(8,128)S(1)} %get-tuple-element.24.own_a), channel_id=1, source_target_pairs={{1,2},{2,1},{3,4},{4,3},{5,6},{6,5},{7,8},{8,7},{9,10},{10,9},{11,... | collective-permute-start | bytes 983048 | tf_op jit(solution)/shard_map/ppermute | solution.py:322
  11.7 3.4 %collective-permute-start = (f32[5,128,128]{2,1,0:T(8,128)S(1)}, f32[5,128,128]{2,1,0:T(8,128)S(1)}, u32[]{:S(2)}, u32[]{:S(2)}) collective-permute-start(f32[5,128,128]{2,1,0:T(8,128)S(1)} %get-tuple-element.22.own_a.own_a1), channel_id=1, source_target_pairs={{1,2},{2,1},{3,4},{4,3},{5,6},{6,5},{7,8},{8,7},{9,10},{10,9},{11,... | collective-permute-start | bytes 983048 | tf_op jit(solution)/shard_map/ppermute | solution.py:322
  15.1 2.8 %collective-permute-done.2.got_a.med_a = f32[5,128,128]{2,1,0:T(8,128)S(1)} collective-permute-done((f32[5,128,128]{2,1,0:T(8,128)S(1)}, f32[5,128,128]{2,1,0:T(8,128)S(1)}, u32[]{:S(2)}, u32[]{:S(2)}) %collective-permute-start.2) | collective-permute-done | bytes 327712 | tf_op jit(solution)/shard_map/ppermute | solution.py:322
  18.4 3.9 %collective-permute-done.got_a.rec_a = f32[5,128,128]{2,1,0:T(8,128)S(1)} collective-permute-done((f32[5,128,128]{2,1,0:T(8,128)S(1)}, f32[5,128,128]{2,1,0:T(8,128)S(1)}, u32[]{:S(2)}, u32[]{:S(2)}) %collective-permute-start) | collective-permute-done | bytes 327712 | tf_op jit(solution)/shard_map/ppermute | solution.py:322
  22.7 1.9 %collective-permute-start.4 = (f32[8,128,128]{2,1,0:T(8,128)S(1)}, f32[8,128,128]{2,1,0:T(8,128)S(1)}, u32[]{:S(2)}, u32[]{:S(2)}) collective-permute-start(f32[8,128,128]{2,1,0:T(8,128)S(1)} %get-tuple-element.28.own_b), channel_id=1, source_target_pairs={{0,1},{1,0},{2,3},{3,2},{4,5},{5,4},{6,7},{7,6},{8,9},{9,8},{10,11... | collective-permute-start | bytes 1572872 | tf_op jit(solution)/shard_map/ppermute | solution.py:329
  24.6 3.5 %collective-permute-start.5 = (f32[4,128,128]{2,1,0:T(8,128)S(1)}, f32[4,128,128]{2,1,0:T(8,128)S(1)}, u32[]{:S(2)}, u32[]{:S(2)}) collective-permute-start(f32[4,128,128]{2,1,0:T(8,128)S(1)} %get-tuple-element.29.own_a), channel_id=1, source_target_pairs={{1,2},{2,1},{3,4},{4,3},{5,6},{6,5},{7,8},{8,7},{9,10},{10,9},{11,... | collective-permute-start | bytes 786440 | tf_op jit(solution)/shard_map/ppermute | solution.py:322
  28.1 4.2 %collective-permute-start.3 = (f32[4,128,128]{2,1,0:T(8,128)S(1)}, f32[4,128,128]{2,1,0:T(8,128)S(1)}, u32[]{:S(2)}, u32[]{:S(2)}) collective-permute-start(f32[4,128,128]{2,1,0:T(8,128)S(1)} %get-tuple-element.27.own_a), channel_id=1, source_target_pairs={{1,2},{2,1},{3,4},{4,3},{5,6},{6,5},{7,8},{8,7},{9,10},{10,9},{11,... | collective-permute-start | bytes 786440 | tf_op jit(solution)/shard_map/ppermute | solution.py:322
  32.3 2.1 %collective-permute-done.5.got_a = f32[4,128,128]{2,1,0:T(8,128)S(1)} collective-permute-done((f32[4,128,128]{2,1,0:T(8,128)S(1)}, f32[4,128,128]{2,1,0:T(8,128)S(1)}, u32[]{:S(2)}, u32[]{:S(2)}) %collective-permute-start.5) | collective-permute-done | bytes 262176 | tf_op jit(solution)/shard_map/ppermute | solution.py:322
  34.9 3.0 %collective-permute-done.3.got_a = f32[4,128,128]{2,1,0:T(8,128)S(1)} collective-permute-done((f32[4,128,128]{2,1,0:T(8,128)S(1)}, f32[4,128,128]{2,1,0:T(8,128)S(1)}, u32[]{:S(2)}, u32[]{:S(2)}) %collective-permute-start.3) | collective-permute-done | bytes 262176 | tf_op jit(solution)/shard_map/ppermute | solution.py:322
  37.9 0.5 shard_map.59
  38.4 1.9 %collective-permute-start.7 = (f32[8,128,128]{2,1,0:T(8,128)S(1)}, f32[8,128,128]{2,1,0:T(8,128)S(1)}, u32[]{:S(2)}, u32[]{:S(2)}) collective-permute-start(f32[8,128,128]{2,1,0:T(8,128)S(1)} %get-tuple-element.32.own_b), channel_id=1, source_target_pairs={{0,1},{1,0},{2,3},{3,2},{4,5},{5,4},{6,7},{7,6},{8,9},{9,8},{10,11... | collective-permute-start | bytes 1572872 | tf_op jit(solution)/shard_map/ppermute | solution.py:329
  40.4 4.2 %collective-permute-start.8 = (f32[4,128,128]{2,1,0:T(8,128)S(1)}, f32[4,128,128]{2,1,0:T(8,128)S(1)}, u32[]{:S(2)}, u32[]{:S(2)}) collective-permute-start(f32[4,128,128]{2,1,0:T(8,128)S(1)} %get-tuple-element.35.own_a), channel_id=1, source_target_pairs={{1,2},{2,1},{3,4},{4,3},{5,6},{6,5},{7,8},{8,7},{9,10},{10,9},{11,... | collective-permute-start | bytes 786440 | tf_op jit(solution)/shard_map/ppermute | solution.py:322
  44.5 3.5 %collective-permute-start.6 = (f32[4,128,128]{2,1,0:T(8,128)S(1)}, f32[4,128,128]{2,1,0:T(8,128)S(1)}, u32[]{:S(2)}, u32[]{:S(2)}) collective-permute-start(f32[4,128,128]{2,1,0:T(8,128)S(1)} %get-tuple-element.31.own_a), channel_id=1, source_target_pairs={{1,2},{2,1},{3,4},{4,3},{5,6},{6,5},{7,8},{8,7},{9,10},{10,9},{11,... | collective-permute-start | bytes 786440 | tf_op jit(solution)/shard_map/ppermute | solution.py:322
  48.1 2.1 %collective-permute-done.8.got_a = f32[4,128,128]{2,1,0:T(8,128)S(1)} collective-permute-done((f32[4,128,128]{2,1,0:T(8,128)S(1)}, f32[4,128,128]{2,1,0:T(8,128)S(1)}, u32[]{:S(2)}, u32[]{:S(2)}) %collective-permute-start.8) | collective-permute-done | bytes 262176 | tf_op jit(solution)/shard_map/ppermute | solution.py:322
  50.5 3.9 %collective-permute-done.6.got_a = f32[4,128,128]{2,1,0:T(8,128)S(1)} collective-permute-done((f32[4,128,128]{2,1,0:T(8,128)S(1)}, f32[4,128,128]{2,1,0:T(8,128)S(1)}, u32[]{:S(2)}, u32[]{:S(2)}) %collective-permute-start.6) | collective-permute-done | bytes 262176 | tf_op jit(solution)/shard_map/ppermute | solution.py:322
  54.7 39.4 %all_to_all.5 = f32[8,2,2,16,128]{4,3,2,1,0:T(8,128)S(1)} all-to-all(f32[8,2,2,16,128]{4,3,2,1,0:T(8,128)S(1)} %shard_map.61), channel_id=1, replica_groups=mesh['freq'=8,'space'=64] {'freq'}, dimensions={0} | all-to-all | bytes 524288 | tf_op jit(solution)/shard_map/all_to_all | solution.py:380
  94.1 0.6 reduce_sum.9
  (13 shorter events, 2.0 us)
Async XLA Ops:
  0.0 0.9 %copy-start = (f32[1,2,2,128,128]{4,3,2,1,0:T(8,128)S(1)}, f32[1,2,2,128,128]{4,3,2,1,0:T(8,128)}, u32[]{:S(2)}) copy-start(f32[1,2,2,128,128]{4,3,2,1,0:T(8,128)} %back_hbm.1) | copy-start | bytes 786436
  1.0 0.9 %copy-start.1 = (f32[2,2,128,128]{3,2,1,0:T(8,128)S(1)}, f32[2,2,128,128]{3,2,1,0:T(8,128)}, u32[]{:S(2)}) copy-start(f32[2,2,128,128]{3,2,1,0:T(8,128)} %probes_hbm.1) | copy-start | bytes 786436
  1.9 0.9 copy-start.2
  2.8 0.9 copy-start.3
  3.7 0.7 copy-start.4
  5.5 12.4 %collective-permute-start.1 = (f32[10,128,128]{2,1,0:T(8,128)S(1)}, f32[10,128,128]{2,1,0:T(8,128)S(1)}, u32[]{:S(2)}, u32[]{:S(2)}) collective-permute-start(f32[10,128,128]{2,1,0:T(8,128)S(1)} %get-tuple-element.23.own_b.own_b1), channel_id=1, source_target_pairs={{0,1},{1,0},{2,3},{3,2},{4,5},{5,4},{6,7},{7,6},{8,9},{9,8},{10,11... | collective-permute-start | bytes 1966088 | tf_op jit(solution)/shard_map/ppermute | solution.py:329
  7.4 10.5 %collective-permute-start.2 = (f32[5,128,128]{2,1,0:T(8,128)S(1)}, f32[5,128,128]{2,1,0:T(8,128)S(1)}, u32[]{:S(2)}, u32[]{:S(2)}) collective-permute-start(f32[5,128,128]{2,1,0:T(8,128)S(1)} %get-tuple-element.24.own_a), channel_id=1, source_target_pairs={{1,2},{2,1},{3,4},{4,3},{5,6},{6,5},{7,8},{8,7},{9,10},{10,9},{11,... | collective-permute-start | bytes 983048 | tf_op jit(solution)/shard_map/ppermute | solution.py:322
  11.7 10.5 %collective-permute-start = (f32[5,128,128]{2,1,0:T(8,128)S(1)}, f32[5,128,128]{2,1,0:T(8,128)S(1)}, u32[]{:S(2)}, u32[]{:S(2)}) collective-permute-start(f32[5,128,128]{2,1,0:T(8,128)S(1)} %get-tuple-element.22.own_a.own_a1), channel_id=1, source_target_pairs={{1,2},{2,1},{3,4},{4,3},{5,6},{6,5},{7,8},{8,7},{9,10},{10,9},{11,... | collective-permute-start | bytes 983048 | tf_op jit(solution)/shard_map/ppermute | solution.py:322
  22.7 11.7 %collective-permute-start.4 = (f32[8,128,128]{2,1,0:T(8,128)S(1)}, f32[8,128,128]{2,1,0:T(8,128)S(1)}, u32[]{:S(2)}, u32[]{:S(2)}) collective-permute-start(f32[8,128,128]{2,1,0:T(8,128)S(1)} %get-tuple-element.28.own_b), channel_id=1, source_target_pairs={{0,1},{1,0},{2,3},{3,2},{4,5},{5,4},{6,7},{7,6},{8,9},{9,8},{10,11... | collective-permute-start | bytes 1572872 | tf_op jit(solution)/shard_map/ppermute | solution.py:329
  24.6 9.8 %collective-permute-start.5 = (f32[4,128,128]{2,1,0:T(8,128)S(1)}, f32[4,128,128]{2,1,0:T(8,128)S(1)}, u32[]{:S(2)}, u32[]{:S(2)}) collective-permute-start(f32[4,128,128]{2,1,0:T(8,128)S(1)} %get-tuple-element.29.own_a), channel_id=1, source_target_pairs={{1,2},{2,1},{3,4},{4,3},{5,6},{6,5},{7,8},{8,7},{9,10},{10,9},{11,... | collective-permute-start | bytes 786440 | tf_op jit(solution)/shard_map/ppermute | solution.py:322
  28.1 9.8 %collective-permute-start.3 = (f32[4,128,128]{2,1,0:T(8,128)S(1)}, f32[4,128,128]{2,1,0:T(8,128)S(1)}, u32[]{:S(2)}, u32[]{:S(2)}) collective-permute-start(f32[4,128,128]{2,1,0:T(8,128)S(1)} %get-tuple-element.27.own_a), channel_id=1, source_target_pairs={{1,2},{2,1},{3,4},{4,3},{5,6},{6,5},{7,8},{8,7},{9,10},{10,9},{11,... | collective-permute-start | bytes 786440 | tf_op jit(solution)/shard_map/ppermute | solution.py:322
  38.4 11.7 %collective-permute-start.7 = (f32[8,128,128]{2,1,0:T(8,128)S(1)}, f32[8,128,128]{2,1,0:T(8,128)S(1)}, u32[]{:S(2)}, u32[]{:S(2)}) collective-permute-start(f32[8,128,128]{2,1,0:T(8,128)S(1)} %get-tuple-element.32.own_b), channel_id=1, source_target_pairs={{0,1},{1,0},{2,3},{3,2},{4,5},{5,4},{6,7},{7,6},{8,9},{9,8},{10,11... | collective-permute-start | bytes 1572872 | tf_op jit(solution)/shard_map/ppermute | solution.py:329
  40.4 9.8 %collective-permute-start.8 = (f32[4,128,128]{2,1,0:T(8,128)S(1)}, f32[4,128,128]{2,1,0:T(8,128)S(1)}, u32[]{:S(2)}, u32[]{:S(2)}) collective-permute-start(f32[4,128,128]{2,1,0:T(8,128)S(1)} %get-tuple-element.35.own_a), channel_id=1, source_target_pairs={{1,2},{2,1},{3,4},{4,3},{5,6},{6,5},{7,8},{8,7},{9,10},{10,9},{11,... | collective-permute-start | bytes 786440 | tf_op jit(solution)/shard_map/ppermute | solution.py:322
  44.5 9.8 %collective-permute-start.6 = (f32[4,128,128]{2,1,0:T(8,128)S(1)}, f32[4,128,128]{2,1,0:T(8,128)S(1)}, u32[]{:S(2)}, u32[]{:S(2)}) collective-permute-start(f32[4,128,128]{2,1,0:T(8,128)S(1)} %get-tuple-element.31.own_a), channel_id=1, source_target_pairs={{1,2},{2,1},{3,4},{4,3},{5,6},{6,5},{7,8},{8,7},{9,10},{10,9},{11,... | collective-permute-start | bytes 786440 | tf_op jit(solution)/shard_map/ppermute | solution.py:322

commit v2 on v1

--- a/solution.py
+++ b/solution.py
@@ -329,6 +329,30 @@
     return lax.ppermute(x, "space", pairs)
 
 
+def halves_kernel(arrived, keep, send):
+    half = lax.rem(lax.axis_index("freq"), 2)
+    count = arrived.shape[0] // 2
+    for out, at in ((keep, half), (send, 1 - half)):
+        for p in range(arrived.shape[1]):
+            for layer in range(arrived.shape[2]):
+                total = arrived[at, p, layer]
+                for k in range(1, count):
+                    total = total + arrived[2 * k + at, p, layer]
+                out[p, layer] = total
+
+
+def reduced(terms):
+    count = lax.axis_size("freq")
+    groups = [list(range(k, count, 2)) for k in range(2)]
+    arrived = lax.all_to_all(
+        terms, "freq", split_axis=0, concat_axis=0, axis_index_groups=groups, tiled=True
+    )
+    shape = terms.shape[1:]
+    keep, send = call(halves_kernel, [shape, shape], [], arrived)
+    pairs = [(k, k ^ 1) for k in range(count)]
+    return keep + lax.ppermute(send, "freq", pairs)
+
+
 def per_device(probes, background, medium, shifts, receivers):
     plane = medium.shape[1:]
     pad = pltpu.VMEM((4, plane[0] + 2 * TOP, plane[1]), jnp.float32)
@@ -340,7 +364,7 @@
         start_kernel,
         [five, five, ten, four, four, (2, 8, plane[1])],
         [pltpu.SMEM(shifts.shape, shifts.dtype), *held, pad, pltpu.SemaphoreType.DMA((5,))],
-        *args,
+        *[pltpu.with_memory_space_constraint(v, pltpu.HBM) for v in args],
         space=pltpu.HBM,
     )
     ra1 = [swap_links(a1[p]) for p in range(2)]
@@ -377,8 +401,7 @@
             row, a3[p], b3[p], ra3[p], rb3, ra1[0], rb1, inv, right[p], waves, *terms,
         )
         terms.append(out)
-    arrived = lax.all_to_all(terms[1], "freq", split_axis=0, concat_axis=0, tiled=True)
-    return arrived.sum(axis=0)
+    return reduced(terms[1])
 
 
 def solution(mesh):

time: 95.2 us -> 84.3 us (0.89)
  the two profiles are of different devices: /device:TPU:32 before, /device:TPU:384 now
where the time goes in v2:
time: 84.3 us; the launch traced here: 83.8 us
  starting transfers between devices  34.3 us (41%)
  waiting for transfers between devices  33.7 us (40%)
  blocking collectives  10.9 us (13%)
  Pallas kernels  4.09 us (5%)
    ppermute x6, starting transfers between devices, swap_links(): return lax.ppermute(x, 'space', pairs)  26.6 us
    ppermute x6, waiting for transfers between devices, swap_links(): return lax.ppermute(x, 'space', pairs)  21.1 us
    ppermute x1, waiting for transfers between devices, reduced(): return keep + lax.ppermute(send, 'freq', pairs)  12.6 us
    all_to_all x1, blocking collectives, reduced(): lax.all_to_all(terms, 'freq', split_axis=0, concat_axis=0, axis_index_gro...  10.9 us
    ppermute x3, starting transfers between devices, swap_cores(): return lax.ppermute(x, 'space', pairs)  5.76 us
    pallas_call x8, Pallas kernels, call(): pl.pallas_call(kernel, out_shape=[jax.ShapeDtypeStruct(s, jnp.float32) fo...  4.09 us
    ppermute x1, starting transfers between devices, reduced(): return keep + lax.ppermute(send, 'freq', pairs)  1.92 us
  transfers between devices with their start and end apart: 10, of which 7 were waited for; matrix products, arithmetic and copies ran while one was open for 0% of the time, Pallas kernels for 1%

profile of v2, /device:TPU:384, one launch (start us, length us, event | category | flops | bytes accessed | tf_op | source)
XLA Modules:
  0.0 83.8 jit_solution(8151447167334999451)
XLA Ops:
  0.0 1.6 %shard_map.55 = (f32[5,128,128]{2,1,0:T(8,128)S(1)}, f32[5,128,128]{2,1,0:T(8,128)S(1)}, f32[10,128,128]{2,1,0:T(8,128)S(1)}, f32[4,128,128]{2,1,0:T(8,128)S(1)}...) custom-call(f32[1,2]{1,0:T(1,128)} %shifts_hbm.1, f32[1,2,2,128,128]{4,3,2,1,0:T(8,128)} %back_hbm.1, ...), custom_call_target="tpu_custom_call" | custom-call | flops 2000000 | bytes 2000000 | tf_op jit(solution)/shard_map/pallas_call | solution.py:306
  1.6 1.9 %collective-permute-start.1 = (f32[10,128,128]{2,1,0:T(8,128)S(1)}, f32[10,128,128]{2,1,0:T(8,128)S(1)}, u32[]{:S(2)}, u32[]{:S(2)}) collective-permute-start(f32[10,128,128]{2,1,0:T(8,128)S(1)} %get-tuple-element.25.own_b.own_b1), channel_id=1, source_target_pairs={{0,1},{1,0},{2,3},{3,2},{4,5},{5,4},{6,7},{7,6},{8,9},{9,8},{10,11... | collective-permute-start | bytes 1966088 | tf_op jit(solution)/shard_map/ppermute | solution.py:329
  3.5 6.4 %collective-permute-start.2 = (f32[5,128,128]{2,1,0:T(8,128)S(1)}, f32[5,128,128]{2,1,0:T(8,128)S(1)}, u32[]{:S(2)}, u32[]{:S(2)}) collective-permute-start(f32[5,128,128]{2,1,0:T(8,128)S(1)} %get-tuple-element.26.own_a), channel_id=1, source_target_pairs={{1,2},{2,1},{3,4},{4,3},{5,6},{6,5},{7,8},{8,7},{9,10},{10,9},{11,... | collective-permute-start | bytes 983048 | tf_op jit(solution)/shard_map/ppermute | solution.py:322
  9.9 2.5 %collective-permute-start = (f32[5,128,128]{2,1,0:T(8,128)S(1)}, f32[5,128,128]{2,1,0:T(8,128)S(1)}, u32[]{:S(2)}, u32[]{:S(2)}) collective-permute-start(f32[5,128,128]{2,1,0:T(8,128)S(1)} %get-tuple-element.24.own_a.own_a1), channel_id=1, source_target_pairs={{1,2},{2,1},{3,4},{4,3},{5,6},{6,5},{7,8},{8,7},{9,10},{10,9},{11,... | collective-permute-start | bytes 983048 | tf_op jit(solution)/shard_map/ppermute | solution.py:322
  12.4 2.8 %collective-permute-done.2.got_a.med_a = f32[5,128,128]{2,1,0:T(8,128)S(1)} collective-permute-done((f32[5,128,128]{2,1,0:T(8,128)S(1)}, f32[5,128,128]{2,1,0:T(8,128)S(1)}, u32[]{:S(2)}, u32[]{:S(2)}) %collective-permute-start.2) | collective-permute-done | bytes 327712 | tf_op jit(solution)/shard_map/ppermute | solution.py:322
  15.2 0.4 shard_map.56
  15.7 6.0 %collective-permute-done.got_a.rec_a = f32[5,128,128]{2,1,0:T(8,128)S(1)} collective-permute-done((f32[5,128,128]{2,1,0:T(8,128)S(1)}, f32[5,128,128]{2,1,0:T(8,128)S(1)}, u32[]{:S(2)}, u32[]{:S(2)}) %collective-permute-start) | collective-permute-done | bytes 327712 | tf_op jit(solution)/shard_map/ppermute | solution.py:322
  21.7 0.5 shard_map.57
  22.1 1.9 %collective-permute-start.4 = (f32[8,128,128]{2,1,0:T(8,128)S(1)}, f32[8,128,128]{2,1,0:T(8,128)S(1)}, u32[]{:S(2)}, u32[]{:S(2)}) collective-permute-start(f32[8,128,128]{2,1,0:T(8,128)S(1)} %get-tuple-element.30.own_b), channel_id=1, source_target_pairs={{0,1},{1,0},{2,3},{3,2},{4,5},{5,4},{6,7},{7,6},{8,9},{9,8},{10,11... | collective-permute-start | bytes 1572872 | tf_op jit(solution)/shard_map/ppermute | solution.py:329
  24.1 3.5 %collective-permute-start.5 = (f32[4,128,128]{2,1,0:T(8,128)S(1)}, f32[4,128,128]{2,1,0:T(8,128)S(1)}, u32[]{:S(2)}, u32[]{:S(2)}) collective-permute-start(f32[4,128,128]{2,1,0:T(8,128)S(1)} %get-tuple-element.31.own_a), channel_id=1, source_target_pairs={{1,2},{2,1},{3,4},{4,3},{5,6},{6,5},{7,8},{8,7},{9,10},{10,9},{11,... | collective-permute-start | bytes 786440 | tf_op jit(solution)/shard_map/ppermute | solution.py:322
  27.6 5.4 %collective-permute-start.3 = (f32[4,128,128]{2,1,0:T(8,128)S(1)}, f32[4,128,128]{2,1,0:T(8,128)S(1)}, u32[]{:S(2)}, u32[]{:S(2)}) collective-permute-start(f32[4,128,128]{2,1,0:T(8,128)S(1)} %get-tuple-element.29.own_a), channel_id=1, source_target_pairs={{1,2},{2,1},{3,4},{4,3},{5,6},{6,5},{7,8},{8,7},{9,10},{10,9},{11,... | collective-permute-start | bytes 786440 | tf_op jit(solution)/shard_map/ppermute | solution.py:322
  32.9 2.1 %collective-permute-done.5.got_a = f32[4,128,128]{2,1,0:T(8,128)S(1)} collective-permute-done((f32[4,128,128]{2,1,0:T(8,128)S(1)}, f32[4,128,128]{2,1,0:T(8,128)S(1)}, u32[]{:S(2)}, u32[]{:S(2)}) %collective-permute-start.5) | collective-permute-done | bytes 262176 | tf_op jit(solution)/shard_map/ppermute | solution.py:322
  35.1 0.5 shard_map.58
  35.6 3.0 %collective-permute-done.3.got_a = f32[4,128,128]{2,1,0:T(8,128)S(1)} collective-permute-done((f32[4,128,128]{2,1,0:T(8,128)S(1)}, f32[4,128,128]{2,1,0:T(8,128)S(1)}, u32[]{:S(2)}, u32[]{:S(2)}) %collective-permute-start.3) | collective-permute-done | bytes 262176 | tf_op jit(solution)/shard_map/ppermute | solution.py:322
  38.6 0.5 shard_map.59
  39.1 1.9 %collective-permute-start.7 = (f32[8,128,128]{2,1,0:T(8,128)S(1)}, f32[8,128,128]{2,1,0:T(8,128)S(1)}, u32[]{:S(2)}, u32[]{:S(2)}) collective-permute-start(f32[8,128,128]{2,1,0:T(8,128)S(1)} %get-tuple-element.34.own_b), channel_id=1, source_target_pairs={{0,1},{1,0},{2,3},{3,2},{4,5},{5,4},{6,7},{7,6},{8,9},{9,8},{10,11... | collective-permute-start | bytes 1572872 | tf_op jit(solution)/shard_map/ppermute | solution.py:329
  41.0 5.4 %collective-permute-start.8 = (f32[4,128,128]{2,1,0:T(8,128)S(1)}, f32[4,128,128]{2,1,0:T(8,128)S(1)}, u32[]{:S(2)}, u32[]{:S(2)}) collective-permute-start(f32[4,128,128]{2,1,0:T(8,128)S(1)} %get-tuple-element.37.own_a), channel_id=1, source_target_pairs={{1,2},{2,1},{3,4},{4,3},{5,6},{6,5},{7,8},{8,7},{9,10},{10,9},{11,... | collective-permute-start | bytes 786440 | tf_op jit(solution)/shard_map/ppermute | solution.py:322
  46.4 3.5 %collective-permute-start.6 = (f32[4,128,128]{2,1,0:T(8,128)S(1)}, f32[4,128,128]{2,1,0:T(8,128)S(1)}, u32[]{:S(2)}, u32[]{:S(2)}) collective-permute-start(f32[4,128,128]{2,1,0:T(8,128)S(1)} %get-tuple-element.33.own_a), channel_id=1, source_target_pairs={{1,2},{2,1},{3,4},{4,3},{5,6},{6,5},{7,8},{8,7},{9,10},{10,9},{11,... | collective-permute-start | bytes 786440 | tf_op jit(solution)/shard_map/ppermute | solution.py:322
  49.9 2.1 %collective-permute-done.8.got_a = f32[4,128,128]{2,1,0:T(8,128)S(1)} collective-permute-done((f32[4,128,128]{2,1,0:T(8,128)S(1)}, f32[4,128,128]{2,1,0:T(8,128)S(1)}, u32[]{:S(2)}, u32[]{:S(2)}) %collective-permute-start.8) | collective-permute-done | bytes 262176 | tf_op jit(solution)/shard_map/ppermute | solution.py:322
  52.3 5.1 %collective-permute-done.6.got_a = f32[4,128,128]{2,1,0:T(8,128)S(1)} collective-permute-done((f32[4,128,128]{2,1,0:T(8,128)S(1)}, f32[4,128,128]{2,1,0:T(8,128)S(1)}, u32[]{:S(2)}, u32[]{:S(2)}) %collective-permute-start.6) | collective-permute-done | bytes 262176 | tf_op jit(solution)/shard_map/ppermute | solution.py:322
  57.7 10.9 %all_to_all.5.arrived = f32[8,2,2,16,128]{4,3,2,1,0:T(8,128)S(1)} all-to-all(f32[8,2,2,16,128]{4,3,2,1,0:T(8,128)S(1)} %shard_map.61), channel_id=1, replica_groups={{0,128,256,384},{64,192,320,448},{1,129,257,385},{65,193,321,449},{2,13..., dimensions={0} | all-to-all | bytes 524288 | tf_op jit(solution)/shard_map/all_to_all | solution.py:347
  68.7 1.9 %collective-permute-start.9 = (f32[2,2,16,128]{3,2,1,0:T(8,128)S(1)}, f32[2,2,16,128]{3,2,1,0:T(8,128)S(1)}, u32[]{:S(2)}, u32[]{:S(2)}) collective-permute-start(f32[2,2,16,128]{3,2,1,0:T(8,128)S(1)} %get-tuple-element.40), channel_id=1, source_target_pairs={{0,64},{64,0},{128,192},{192,128},{256,320},{320,256},{384,448},{4... | collective-permute-start | bytes 98312 | tf_op jit(solution)/shard_map/ppermute | solution.py:353
  70.6 12.6 %collective-permute-done.9 = f32[2,2,16,128]{3,2,1,0:T(8,128)S(1)} collective-permute-done((f32[2,2,16,128]{3,2,1,0:T(8,128)S(1)}, f32[2,2,16,128]{3,2,1,0:T(8,128)S(1)}, u32[]{:S(2)}, u32[]{:S(2)}) %collective-permute-start.9) | collective-permute-done | bytes 32800 | tf_op jit(solution)/shard_map/ppermute | solution.py:353
  83.2 0.6 add.3
  (6 shorter events, 0.6 us)
Async XLA Ops:
  1.6 13.6 %collective-permute-start.1 = (f32[10,128,128]{2,1,0:T(8,128)S(1)}, f32[10,128,128]{2,1,0:T(8,128)S(1)}, u32[]{:S(2)}, u32[]{:S(2)}) collective-permute-start(f32[10,128,128]{2,1,0:T(8,128)S(1)} %get-tuple-element.25.own_b.own_b1), channel_id=1, source_target_pairs={{0,1},{1,0},{2,3},{3,2},{4,5},{5,4},{6,7},{7,6},{8,9},{9,8},{10,11... | collective-permute-start | bytes 1966088 | tf_op jit(solution)/shard_map/ppermute | solution.py:329
  3.5 11.7 %collective-permute-start.2 = (f32[5,128,128]{2,1,0:T(8,128)S(1)}, f32[5,128,128]{2,1,0:T(8,128)S(1)}, u32[]{:S(2)}, u32[]{:S(2)}) collective-permute-start(f32[5,128,128]{2,1,0:T(8,128)S(1)} %get-tuple-element.26.own_a), channel_id=1, source_target_pairs={{1,2},{2,1},{3,4},{4,3},{5,6},{6,5},{7,8},{8,7},{9,10},{10,9},{11,... | collective-permute-start | bytes 983048 | tf_op jit(solution)/shard_map/ppermute | solution.py:322
  9.9 11.7 %collective-permute-start = (f32[5,128,128]{2,1,0:T(8,128)S(1)}, f32[5,128,128]{2,1,0:T(8,128)S(1)}, u32[]{:S(2)}, u32[]{:S(2)}) collective-permute-start(f32[5,128,128]{2,1,0:T(8,128)S(1)} %get-tuple-element.24.own_a.own_a1), channel_id=1, source_target_pairs={{1,2},{2,1},{3,4},{4,3},{5,6},{6,5},{7,8},{8,7},{9,10},{10,9},{11,... | collective-permute-start | bytes 983048 | tf_op jit(solution)/shard_map/ppermute | solution.py:322
  22.1 12.9 %collective-permute-start.4 = (f32[8,128,128]{2,1,0:T(8,128)S(1)}, f32[8,128,128]{2,1,0:T(8,128)S(1)}, u32[]{:S(2)}, u32[]{:S(2)}) collective-permute-start(f32[8,128,128]{2,1,0:T(8,128)S(1)} %get-tuple-element.30.own_b), channel_id=1, source_target_pairs={{0,1},{1,0},{2,3},{3,2},{4,5},{5,4},{6,7},{7,6},{8,9},{9,8},{10,11... | collective-permute-start | bytes 1572872 | tf_op jit(solution)/shard_map/ppermute | solution.py:329
  24.1 11.0 %collective-permute-start.5 = (f32[4,128,128]{2,1,0:T(8,128)S(1)}, f32[4,128,128]{2,1,0:T(8,128)S(1)}, u32[]{:S(2)}, u32[]{:S(2)}) collective-permute-start(f32[4,128,128]{2,1,0:T(8,128)S(1)} %get-tuple-element.31.own_a), channel_id=1, source_target_pairs={{1,2},{2,1},{3,4},{4,3},{5,6},{6,5},{7,8},{8,7},{9,10},{10,9},{11,... | collective-permute-start | bytes 786440 | tf_op jit(solution)/shard_map/ppermute | solution.py:322
  27.6 11.0 %collective-permute-start.3 = (f32[4,128,128]{2,1,0:T(8,128)S(1)}, f32[4,128,128]{2,1,0:T(8,128)S(1)}, u32[]{:S(2)}, u32[]{:S(2)}) collective-permute-start(f32[4,128,128]{2,1,0:T(8,128)S(1)} %get-tuple-element.29.own_a), channel_id=1, source_target_pairs={{1,2},{2,1},{3,4},{4,3},{5,6},{6,5},{7,8},{8,7},{9,10},{10,9},{11,... | collective-permute-start | bytes 786440 | tf_op jit(solution)/shard_map/ppermute | solution.py:322
  39.1 12.9 %collective-permute-start.7 = (f32[8,128,128]{2,1,0:T(8,128)S(1)}, f32[8,128,128]{2,1,0:T(8,128)S(1)}, u32[]{:S(2)}, u32[]{:S(2)}) collective-permute-start(f32[8,128,128]{2,1,0:T(8,128)S(1)} %get-tuple-element.34.own_b), channel_id=1, source_target_pairs={{0,1},{1,0},{2,3},{3,2},{4,5},{5,4},{6,7},{7,6},{8,9},{9,8},{10,11... | collective-permute-start | bytes 1572872 | tf_op jit(solution)/shard_map/ppermute | solution.py:329
  41.0 11.0 %collective-permute-start.8 = (f32[4,128,128]{2,1,0:T(8,128)S(1)}, f32[4,128,128]{2,1,0:T(8,128)S(1)}, u32[]{:S(2)}, u32[]{:S(2)}) collective-permute-start(f32[4,128,128]{2,1,0:T(8,128)S(1)} %get-tuple-element.37.own_a), channel_id=1, source_target_pairs={{1,2},{2,1},{3,4},{4,3},{5,6},{6,5},{7,8},{8,7},{9,10},{10,9},{11,... | collective-permute-start | bytes 786440 | tf_op jit(solution)/shard_map/ppermute | solution.py:322
  46.4 11.0 %collective-permute-start.6 = (f32[4,128,128]{2,1,0:T(8,128)S(1)}, f32[4,128,128]{2,1,0:T(8,128)S(1)}, u32[]{:S(2)}, u32[]{:S(2)}) collective-permute-start(f32[4,128,128]{2,1,0:T(8,128)S(1)} %get-tuple-element.33.own_a), channel_id=1, source_target_pairs={{1,2},{2,1},{3,4},{4,3},{5,6},{6,5},{7,8},{8,7},{9,10},{10,9},{11,... | collective-permute-start | bytes 786440 | tf_op jit(solution)/shard_map/ppermute | solution.py:322
  68.7 14.5 %collective-permute-start.9 = (f32[2,2,16,128]{3,2,1,0:T(8,128)S(1)}, f32[2,2,16,128]{3,2,1,0:T(8,128)S(1)}, u32[]{:S(2)}, u32[]{:S(2)}) collective-permute-start(f32[2,2,16,128]{3,2,1,0:T(8,128)S(1)} %get-tuple-element.40), channel_id=1, source_target_pairs={{0,64},{64,0},{128,192},{192,128},{256,320},{320,256},{384,448},{4... | collective-permute-start | bytes 98312 | tf_op jit(solution)/shard_map/ppermute | solution.py:353

commit v3 on v2

--- a/solution.py
+++ b/solution.py
@@ -83,6 +83,16 @@
     at = lax.axis_index("space")
     last = lax.axis_size("space") - 1
     return jnp.where((at == 0) | (at == last), 0.0, 1.0).astype(jnp.float32)
+
+
+def probe_at(parts, p):
+    ref, at = parts[p]
+    return (ref, at + 2) if p == 0 else (ref, at)
+
+
+def first_of(parts, p, r, n):
+    (gain, gain_at), (ref, at) = parts[0], probe_at(parts, p)
+    return scale(ref[at, r : r + n], load(gain, gain_at, r, n))
 
 
 def start_kernel(
@@ -107,7 +117,7 @@
     near = side()
     own = (near, 1 - near)
     height = medium.shape[1]
-    outs = ((out_a0, 0), (out_a1, 0)), ((out_b, 0), (out_b, 5))
+    outs = ((out_a0, 0), (out_a1, 0)), ((out_b, 0), (out_b, 6))
     clear_edges(pad)
     copies[0].wait()
     shift_re, shift_im = shifts[0, 0], shifts[0, 1]
@@ -118,34 +128,37 @@
         for r, n in chunks(height):
             med = medium[own[layer], r : r + n]
             store(inv, 2 * layer, r, n, inverse(med, shift_re, shift_im))
-            outs[layer][0][0][outs[layer][0][1] + 4, r : r + n] = med
+            outs[layer][0][0][outs[layer][0][1] + 5, r : r + n] = med
     copies[2].wait()
     for layer in range(2):
+        ref, at = outs[layer][0]
         for r, n in chunks(height):
             rows = slice(r, r + n)
             bg = (back[0, 0, own[layer], rows], back[0, 1, own[layer], rows])
-            store(waves, 2 * layer, r, n, multiply((shift_re, shift_im), bg))
+            wave = multiply((shift_re, shift_im), bg)
+            store(waves, 2 * layer, r, n, wave)
+            store(ref, at, r, n, multiply(load(inv, 2 * layer, r, n), wave))
     copies[3].wait()
     for p in range(2):
         for layer in range(2):
-            ref, at = outs[layer][p]
+            gain, gain_at = outs[layer][0]
+            ref, at = probe_at(outs[layer], p)
             for r, n in chunks(height):
                 probe = probes[p, own[layer], r : r + n]
-                first = scale(probe, multiply(load(inv, 2 * layer, r, n), load(waves, 2 * layer, r, n)))
-                store(ref, at, r, n, first)
-                store(pad, 2 * layer, TOP + r, n, first)
+                ref[at, r : r + n] = probe
+                store(pad, 2 * layer, TOP + r, n, scale(probe, load(gain, gain_at, r, n)))
         for layer in range(2):
-            ref, at = outs[layer][p]
+            ref, at = probe_at(outs[layer], p)
             for r, n in chunks(height):
                 here, around = complex_in_plane(pad, layer, r, n)
                 around = add(around, load(pad, 2 * (1 - layer), TOP + r, n))
                 part = add(scale(1.0 + KEEP, here), multiply(load(inv, 2 * layer, r, n), around))
-                store(ref, at + 2, r, n, part)
+                store(ref, at + 1, r, n, part)
     copies[4].wait()
     for layer in range(2):
         ref, at = outs[layer][1]
         for r, n in chunks(height):
-            ref[at + 4, r : r + n] = receivers[own[layer], r : r + n].astype(jnp.float32)
+            ref[at + 3, r : r + n] = receivers[own[layer], r : r + n].astype(jnp.float32)
 
 
 def halo_inverse(med, layer, row, mask):
@@ -153,36 +166,36 @@
     return (mask * re, mask * im) if layer == 0 else (re, im)
 
 
-def forward_kernel(p, row, own_a, own_b, got_a, got_b, med_a, inv, *rest):
+def forward_kernel(p, row, own_a0, own_a, own_b, got_a0, got_a, got_b, inv, *rest):
     if p == 0:
         out_a, out_b, pad, spare = rest
-        b_at, out_at = 0, 0
+        out_at = 0
     else:
         first_b, out_a, out_b, pad, spare = rest
-        b_at, out_at = 5, 4
+        out_at = 4
         out_b[0:4] = first_b[...]
     mask = has_partner()
     height = inv.shape[1]
-    own = ((own_a, 0), (own_b, b_at))
-    got = ((got_a, 0), (got_b, b_at))
-    med = ((med_a, 4), (got_b, 4))
+    own = ((own_a0, 0), (own_a, 0)), ((own_b, 0), (own_b, 6))
+    got = ((got_a0, 0), (got_a, 0)), ((got_b, 0), (got_b, 6))
     out = ((out_a, 0), (out_b, out_at))
     clear_edges(pad)
     clear_edges(spare)
     for layer in range(2):
-        (mine, at), (theirs, from_) = own[layer], got[layer]
+        mine, at = probe_at(own[layer], p)
         for r, n in chunks(height):
             second = add(
-                load(mine, at + 2, r, n),
-                multiply(load(inv, 2 * layer, r, n), load(theirs, from_, r, n)),
+                load(mine, at + 1, r, n),
+                multiply(load(inv, 2 * layer, r, n), first_of(got[layer], p, r, n)),
             )
             store(pad, 2 * layer, TOP + r, n, second)
     for layer in range(2):
-        (mine, at), (theirs, from_) = own[layer], got[layer]
-        for r, n in chunks(height):
-            first = load(mine, at, r, n)
-            there = halo_inverse(med[layer][0][med[layer][1], r : r + n], layer, row, mask)
-            halo = add(load(theirs, from_ + 2, r, n), multiply(there, first))
+        theirs, from_ = probe_at(got[layer], p)
+        med, med_at = got[layer][0]
+        for r, n in chunks(height):
+            first = first_of(own[layer], p, r, n)
+            there = halo_inverse(med[med_at + 5, r : r + n], layer, row, mask)
+            halo = add(load(theirs, from_ + 1, r, n), multiply(there, first))
             here, around = complex_in_plane(pad, layer, r, n)
             around = add(add(around, halo), load(pad, 2 * (1 - layer), TOP + r, n))
             third = add(
@@ -191,12 +204,11 @@
             store(spare, 2 * layer, TOP + r, n, third)
             store(out[layer][0], out[layer][1], r, n, third)
     for layer in range(2):
-        mine, at = own[layer]
         for r, n in chunks(height):
             here, around = complex_in_plane(spare, layer, r, n)
             around = add(around, load(spare, 2 * (1 - layer), TOP + r, n))
             part = add(
-                add(scale(KEEP, here), load(mine, at, r, n)),
+                add(scale(KEEP, here), first_of(own[layer], p, r, n)),
                 multiply(load(inv, 2 * layer, r, n), around),
             )
             store(out[layer][0], out[layer][1] + 2, r, n, part)
@@ -206,19 +218,20 @@
     p, row, own_a, own_b, got_a, got_b, med_a, got_b1, rec_a, own_a1, own_b1, inv, *rest
 ):
     if p == 0:
-        out_a, out_b, right, pad, spare = rest
+        out_a, out_b, right, part_sum, pad, spare = rest
         b_at, out_at = 0, 0
     else:
-        first_b, out_a, out_b, right, pad, spare = rest
-        b_at, out_at = 4, 4
-        out_b[0:4] = first_b[...]
+        first_b, out_a, out_b, right, part_sum, pad, spare = rest
+        b_at, out_at = 4, 3
+        out_b[0:3] = first_b[...]
     mask = has_partner()
     height = inv.shape[1]
     own = ((own_a, 0), (own_b, 0 if p == 0 else b_at))
     got = ((got_a, 0), (got_b, b_at))
-    med = ((med_a, 4), (got_b1, 4))
-    rec_own = ((own_a1, 4), (own_b1, 9))
-    rec_got = ((rec_a, 4), (got_b1, 9))
+    med = ((med_a, 5), (got_b1, 5))
+    rec_own = ((own_a1, 3), (own_b1, 9))
+    rec_got = ((rec_a, 3), (got_b1, 9))
+    gain = (med_a, got_b1)
     out = ((out_a, 0), (out_b, out_at))
     clear_edges(pad)
     clear_edges(spare)
@@ -254,16 +267,18 @@
                 add(scale(KEEP, here), load(right, 2 * layer, r, n)),
                 multiply_conj(load(inv, 2 * layer, r, n), around),
             )
-            store(out[layer][0], out[layer][1] + 2, r, n, part)
-
-
-def end_kernel(p, row, own_a, own_b, got_a, got_b, med_a, got_b1, inv, right, waves, *rest):
+            store(part_sum, 2 * layer, r, n, part)
+            seen = load(gain[layer], 0, r, n)
+            out[layer][0][out[layer][1] + 2, r : r + n] = seen[0] * part[0] + seen[1] * part[1]
+
+
+def end_kernel(p, row, own_a, own_b, got_a, got_b, med_a, got_b1, inv, right, part_sum, waves, own_a1, own_b1, *rest):
     if p == 0:
         out, pad = rest
         b_at, out_at = 0, 0
     else:
         first_out, out, pad = rest
-        b_at, out_at = 4, 1
+        b_at, out_at = 3, 1
         out[:, 0:1] = first_out[...]
     mask = has_partner()
     near = side()
@@ -272,13 +287,14 @@
     strip = out.shape[3]
     own = ((own_a, 0), (own_b, 0 if p == 0 else b_at))
     got = ((got_a, 0), (got_b, b_at))
-    med = ((med_a, 4), (got_b1, 4))
+    med = ((med_a, 5), (got_b1, 5))
+    gain = (own_a1, own_b1)
     clear_edges(pad)
     for layer in range(2):
         (mine, at), (theirs, from_) = own[layer], got[layer]
         for r, n in chunks(height):
             third = add(
-                load(mine, at + 2, r, n),
+                load(part_sum, 2 * layer, r, n),
                 multiply_conj(load(inv, 2 * layer, r, n), load(theirs, from_, r, n)),
             )
             store(pad, 2 * layer, TOP + r, n, third)
@@ -286,17 +302,17 @@
         (mine, at), (theirs, from_) = own[layer], got[layer]
         for r, n in chunks(height):
             there = halo_inverse(med[layer][0][med[layer][1], r : r + n], layer, row, mask)
-            halo = add(
-                load(theirs, from_ + 2, r, n), multiply_conj(there, load(mine, at, r, n))
-            )
+            halo = multiply_conj(there, load(mine, at, r, n))
+            seen = load(gain[layer], 0, r, n)
+            across = theirs[from_ + 2, r : r + n] + (seen[0] * halo[0] + seen[1] * halo[1])
             here, around = complex_in_plane(pad, layer, r, n)
-            around = add(add(around, halo), load(pad, 2 * (1 - layer), TOP + r, n))
+            around = add(around, load(pad, 2 * (1 - layer), TOP + r, n))
             fourth = add(
                 add(scale(KEEP, here), load(right, 2 * layer, r, n)),
                 multiply_conj(load(inv, 2 * layer, r, n), around),
             )
             wave = load(waves, 2 * layer, r, n)
-            term = wave[0] * fourth[0] + wave[1] * fourth[1]
+            term = (wave[0] * fourth[0] + wave[1] * fourth[1]) + across
             for k in range(0, n, strip):
                 out[(r + k) // strip, out_at, place[layer]] = term[k : k + strip]
 
@@ -356,13 +372,13 @@
 def per_device(probes, background, medium, shifts, receivers):
     plane = medium.shape[1:]
     pad = pltpu.VMEM((4, plane[0] + 2 * TOP, plane[1]), jnp.float32)
-    five, ten, four, eight = [(k, *plane) for k in (5, 10, 4, 8)]
+    three, four, six, eight, ten = [(k, *plane) for k in (3, 4, 6, 8, 10)]
     args = (shifts, background, probes, medium, receivers)
     held = [pltpu.VMEM(v.shape, v.dtype) for v in args[1:]]
     a1 = [None, None]
     a1[0], a1[1], b1, inv, waves, row = call(
         start_kernel,
-        [five, five, ten, four, four, (2, 8, plane[1])],
+        [six, four, ten, four, four, (2, 8, plane[1])],
         [pltpu.SMEM(shifts.shape, shifts.dtype), *held, pad, pltpu.SemaphoreType.DMA((5,))],
         *[pltpu.with_memory_space_constraint(v, pltpu.HBM) for v in args],
         space=pltpu.HBM,
@@ -375,16 +391,17 @@
             functools.partial(forward_kernel, p),
             [four, eight if p else four],
             [pad, pad],
-            row, a1[p], b1, ra1[p], rb1, ra1[0], inv, *b2,
+            row, a1[0], a1[p], b1, ra1[0], ra1[p], rb1, inv, *b2,
         )
         b2.append(out_b)
         ra2[p] = swap_links(a2[p])
     rb2 = swap_cores(b2[1])
-    a3, ra3, b3, right = [None, None], [None, None], [], [None, None]
+    a3, ra3, b3 = [None, None], [None, None], []
+    right, part_sum = [None, None], [None, None]
     for p in range(2):
-        a3[p], out_b, right[p] = call(
+        a3[p], out_b, right[p], part_sum[p] = call(
             functools.partial(turn_kernel, p),
-            [four, eight if p else four, four],
+            [three, six if p else three, four, four],
             [pad, pad],
             row, a2[p], b2[p], ra2[p], rb2, ra1[0], rb1, ra1[1], a1[1], b1, inv, *b3,
         )
@@ -398,7 +415,8 @@
             functools.partial(end_kernel, p),
             [(blocks, p + 1, 2, plane[0] // blocks, plane[1])],
             [pad],
-            row, a3[p], b3[p], ra3[p], rb3, ra1[0], rb1, inv, right[p], waves, *terms,
+            row, a3[p], b3[p], ra3[p], rb3, ra1[0], rb1, inv, right[p], part_sum[p],
+            waves, a1[0], b1, *terms,
         )
         terms.append(out)
     return reduced(terms[1])

time: 84.3 us -> 82.8 us (0.982)
  waiting for transfers between devices: 33.7 us -> 32.3 us
    ppermute x6, waiting for transfers between devices: 21.1 us -> 19.7 us  [swap_links(): return lax.ppermute(x, 'space', pairs)]
  transfers between devices with their start and end apart: 10 -> 10, of which waited for: 7 -> 7; matrix products, arithmetic and copies ran while one was open for 0% -> 0% of each run, Pallas kernels for 1% -> 2%
where the time goes in v3:
time: 82.8 us; the launch traced here: 82.4 us
  starting transfers between devices  34.3 us (41%)
  waiting for transfers between devices  32.3 us (39%)
  blocking collectives  10.9 us (13%)
  Pallas kernels  4.07 us (5%)
    ppermute x6, starting transfers between devices, swap_links(): return lax.ppermute(x, 'space', pairs)  26.6 us
    ppermute x6, waiting for transfers between devices, swap_links(): return lax.ppermute(x, 'space', pairs)  19.7 us
    ppermute x1, waiting for transfers between devices, reduced(): return keep + lax.ppermute(send, 'freq', pairs)  12.6 us
    all_to_all x1, blocking collectives, reduced(): lax.all_to_all(terms, 'freq', split_axis=0, concat_axis=0, axis_index_gro...  10.9 us
    ppermute x3, starting transfers between devices, swap_cores(): return lax.ppermute(x, 'space', pairs)  5.76 us
    pallas_call x8, Pallas kernels, call(): pl.pallas_call(kernel, out_shape=[jax.ShapeDtypeStruct(s, jnp.float32) fo...  4.07 us
    ppermute x1, starting transfers between devices, reduced(): return keep + lax.ppermute(send, 'freq', pairs)  1.92 us
  transfers between devices with their start and end apart: 10, of which 7 were waited for; matrix products, arithmetic and copies ran while one was open for 0% of the time, Pallas kernels for 2%

profile of v3, /device:TPU:384, one launch (start us, length us, event | category | flops | bytes accessed | tf_op | source)
XLA Modules:
  0.0 82.4 jit_solution(11198359448161459626)
XLA Ops:
  0.0 1.5 %shard_map.55 = (f32[6,128,128]{2,1,0:T(8,128)S(1)}, f32[4,128,128]{2,1,0:T(8,128)S(1)}, f32[10,128,128]{2,1,0:T(8,128)S(1)}, f32[4,128,128]{2,1,0:T(8,128)S(1)}...) custom-call(f32[1,2]{1,0:T(1,128)} %shifts_hbm.1, f32[1,2,2,128,128]{4,3,2,1,0:T(8,128)} %back_hbm.1, ...), custom_call_target="tpu_custom_call" | custom-call | flops 2000000 | bytes 2000000 | tf_op jit(solution)/shard_map/pallas_call | solution.py:322
  1.5 1.9 %collective-permute-start.2 = (f32[10,128,128]{2,1,0:T(8,128)S(1)}, f32[10,128,128]{2,1,0:T(8,128)S(1)}, u32[]{:S(2)}, u32[]{:S(2)}) collective-permute-start(f32[10,128,128]{2,1,0:T(8,128)S(1)} %get-tuple-element.28.own_b.own_b1), channel_id=1, source_target_pairs={{0,1},{1,0},{2,3},{3,2},{4,5},{5,4},{6,7},{7,6},{8,9},{9,8},{10,11... | collective-permute-start | bytes 1966088 | tf_op jit(solution)/shard_map/ppermute | solution.py:345
  3.4 6.4 %collective-permute-start = (f32[6,128,128]{2,1,0:T(8,128)S(1)}, f32[6,128,128]{2,1,0:T(8,128)S(1)}, u32[]{:S(2)}, u32[]{:S(2)}) collective-permute-start(f32[6,128,128]{2,1,0:T(8,128)S(1)} %get-tuple-element.26.own_a0.own_a.own_a1), channel_id=1, source_target_pairs={{1,2},{2,1},{3,4},{4,3},{5,6},{6,5},{7,8},{8,7},{9,10},{10,9},{11,... | collective-permute-start | bytes 1179656 | tf_op jit(solution)/shard_map/ppermute | solution.py:338
  9.9 2.5 %collective-permute-start.1 = (f32[4,128,128]{2,1,0:T(8,128)S(1)}, f32[4,128,128]{2,1,0:T(8,128)S(1)}, u32[]{:S(2)}, u32[]{:S(2)}) collective-permute-start(f32[4,128,128]{2,1,0:T(8,128)S(1)} %get-tuple-element.27.own_a.own_a1), channel_id=1, source_target_pairs={{1,2},{2,1},{3,4},{4,3},{5,6},{6,5},{7,8},{8,7},{9,10},{10,9},{11,... | collective-permute-start | bytes 786440 | tf_op jit(solution)/shard_map/ppermute | solution.py:338
  12.3 3.5 %collective-permute-done.got_a0.got_a.med_a = f32[6,128,128]{2,1,0:T(8,128)S(1)} collective-permute-done((f32[6,128,128]{2,1,0:T(8,128)S(1)}, f32[6,128,128]{2,1,0:T(8,128)S(1)}, u32[]{:S(2)}, u32[]{:S(2)}) %collective-permute-start) | collective-permute-done | bytes 393248 | tf_op jit(solution)/shard_map/ppermute | solution.py:338
  15.9 0.4 shard_map.56
  16.3 4.6 %collective-permute-done.1.got_a.rec_a = f32[4,128,128]{2,1,0:T(8,128)S(1)} collective-permute-done((f32[4,128,128]{2,1,0:T(8,128)S(1)}, f32[4,128,128]{2,1,0:T(8,128)S(1)}, u32[]{:S(2)}, u32[]{:S(2)}) %collective-permute-start.1) | collective-permute-done | bytes 262176 | tf_op jit(solution)/shard_map/ppermute | solution.py:338
  20.9 0.5 shard_map.57
  21.4 1.9 %collective-permute-start.4 = (f32[8,128,128]{2,1,0:T(8,128)S(1)}, f32[8,128,128]{2,1,0:T(8,128)S(1)}, u32[]{:S(2)}, u32[]{:S(2)}) collective-permute-start(f32[8,128,128]{2,1,0:T(8,128)S(1)} %get-tuple-element.32.own_b), channel_id=1, source_target_pairs={{0,1},{1,0},{2,3},{3,2},{4,5},{5,4},{6,7},{7,6},{8,9},{9,8},{10,11... | collective-permute-start | bytes 1572872 | tf_op jit(solution)/shard_map/ppermute | solution.py:345
  23.3 4.2 %collective-permute-start.5 = (f32[4,128,128]{2,1,0:T(8,128)S(1)}, f32[4,128,128]{2,1,0:T(8,128)S(1)}, u32[]{:S(2)}, u32[]{:S(2)}) collective-permute-start(f32[4,128,128]{2,1,0:T(8,128)S(1)} %get-tuple-element.33.own_a), channel_id=1, source_target_pairs={{1,2},{2,1},{3,4},{4,3},{5,6},{6,5},{7,8},{8,7},{9,10},{10,9},{11,... | collective-permute-start | bytes 786440 | tf_op jit(solution)/shard_map/ppermute | solution.py:338
  27.5 4.7 %collective-permute-start.3 = (f32[4,128,128]{2,1,0:T(8,128)S(1)}, f32[4,128,128]{2,1,0:T(8,128)S(1)}, u32[]{:S(2)}, u32[]{:S(2)}) collective-permute-start(f32[4,128,128]{2,1,0:T(8,128)S(1)} %get-tuple-element.31.own_a), channel_id=1, source_target_pairs={{1,2},{2,1},{3,4},{4,3},{5,6},{6,5},{7,8},{8,7},{9,10},{10,9},{11,... | collective-permute-start | bytes 786440 | tf_op jit(solution)/shard_map/ppermute | solution.py:338
  32.2 2.1 %collective-permute-done.5.got_a = f32[4,128,128]{2,1,0:T(8,128)S(1)} collective-permute-done((f32[4,128,128]{2,1,0:T(8,128)S(1)}, f32[4,128,128]{2,1,0:T(8,128)S(1)}, u32[]{:S(2)}, u32[]{:S(2)}) %collective-permute-start.5) | collective-permute-done | bytes 262176 | tf_op jit(solution)/shard_map/ppermute | solution.py:338
  34.3 0.5 shard_map.58
  34.8 3.7 %collective-permute-done.3.got_a = f32[4,128,128]{2,1,0:T(8,128)S(1)} collective-permute-done((f32[4,128,128]{2,1,0:T(8,128)S(1)}, f32[4,128,128]{2,1,0:T(8,128)S(1)}, u32[]{:S(2)}, u32[]{:S(2)}) %collective-permute-start.3) | collective-permute-done | bytes 262176 | tf_op jit(solution)/shard_map/ppermute | solution.py:338
  38.5 0.5 shard_map.59
  39.0 1.9 %collective-permute-start.7 = (f32[6,128,128]{2,1,0:T(8,128)S(1)}, f32[6,128,128]{2,1,0:T(8,128)S(1)}, u32[]{:S(2)}, u32[]{:S(2)}) collective-permute-start(f32[6,128,128]{2,1,0:T(8,128)S(1)} %get-tuple-element.36.own_b), channel_id=1, source_target_pairs={{0,1},{1,0},{2,3},{3,2},{4,5},{5,4},{6,7},{7,6},{8,9},{9,8},{10,11... | collective-permute-start | bytes 1179656 | tf_op jit(solution)/shard_map/ppermute | solution.py:345
  41.0 4.7 %collective-permute-start.8 = (f32[3,128,128]{2,1,0:T(8,128)S(1)}, f32[3,128,128]{2,1,0:T(8,128)S(1)}, u32[]{:S(2)}, u32[]{:S(2)}) collective-permute-start(f32[3,128,128]{2,1,0:T(8,128)S(1)} %get-tuple-element.40.own_a), channel_id=1, source_target_pairs={{1,2},{2,1},{3,4},{4,3},{5,6},{6,5},{7,8},{8,7},{9,10},{10,9},{11,... | collective-permute-start | bytes 589832 | tf_op jit(solution)/shard_map/ppermute | solution.py:338
  45.6 4.2 %collective-permute-start.6 = (f32[3,128,128]{2,1,0:T(8,128)S(1)}, f32[3,128,128]{2,1,0:T(8,128)S(1)}, u32[]{:S(2)}, u32[]{:S(2)}) collective-permute-start(f32[3,128,128]{2,1,0:T(8,128)S(1)} %get-tuple-element.35.own_a), channel_id=1, source_target_pairs={{1,2},{2,1},{3,4},{4,3},{5,6},{6,5},{7,8},{8,7},{9,10},{10,9},{11,... | collective-permute-start | bytes 589832 | tf_op jit(solution)/shard_map/ppermute | solution.py:338
  49.9 1.4 %collective-permute-done.8.got_a = f32[3,128,128]{2,1,0:T(8,128)S(1)} collective-permute-done((f32[3,128,128]{2,1,0:T(8,128)S(1)}, f32[3,128,128]{2,1,0:T(8,128)S(1)}, u32[]{:S(2)}, u32[]{:S(2)}) %collective-permute-start.8) | collective-permute-done | bytes 196640 | tf_op jit(solution)/shard_map/ppermute | solution.py:338
  51.6 4.4 %collective-permute-done.6.got_a = f32[3,128,128]{2,1,0:T(8,128)S(1)} collective-permute-done((f32[3,128,128]{2,1,0:T(8,128)S(1)}, f32[3,128,128]{2,1,0:T(8,128)S(1)}, u32[]{:S(2)}, u32[]{:S(2)}) %collective-permute-start.6) | collective-permute-done | bytes 196640 | tf_op jit(solution)/shard_map/ppermute | solution.py:338
  56.3 10.9 %all_to_all.5.arrived = f32[8,2,2,16,128]{4,3,2,1,0:T(8,128)S(1)} all-to-all(f32[8,2,2,16,128]{4,3,2,1,0:T(8,128)S(1)} %shard_map.61), channel_id=1, replica_groups={{0,128,256,384},{64,192,320,448},{1,129,257,385},{65,193,321,449},{2,13..., dimensions={0} | all-to-all | bytes 524288 | tf_op jit(solution)/shard_map/all_to_all | solution.py:363
  67.2 1.9 %collective-permute-start.9 = (f32[2,2,16,128]{3,2,1,0:T(8,128)S(1)}, f32[2,2,16,128]{3,2,1,0:T(8,128)S(1)}, u32[]{:S(2)}, u32[]{:S(2)}) collective-permute-start(f32[2,2,16,128]{3,2,1,0:T(8,128)S(1)} %get-tuple-element.44), channel_id=1, source_target_pairs={{0,64},{64,0},{128,192},{192,128},{256,320},{320,256},{384,448},{4... | collective-permute-start | bytes 98312 | tf_op jit(solution)/shard_map/ppermute | solution.py:369
  69.2 12.6 %collective-permute-done.9 = f32[2,2,16,128]{3,2,1,0:T(8,128)S(1)} collective-permute-done((f32[2,2,16,128]{3,2,1,0:T(8,128)S(1)}, f32[2,2,16,128]{3,2,1,0:T(8,128)S(1)}, u32[]{:S(2)}, u32[]{:S(2)}) %collective-permute-start.9) | collective-permute-done | bytes 32800 | tf_op jit(solution)/shard_map/ppermute | solution.py:369
  81.8 0.6 add.3
  (6 shorter events, 0.7 us)
Async XLA Ops:
  1.5 14.3 %collective-permute-start.2 = (f32[10,128,128]{2,1,0:T(8,128)S(1)}, f32[10,128,128]{2,1,0:T(8,128)S(1)}, u32[]{:S(2)}, u32[]{:S(2)}) collective-permute-start(f32[10,128,128]{2,1,0:T(8,128)S(1)} %get-tuple-element.28.own_b.own_b1), channel_id=1, source_target_pairs={{0,1},{1,0},{2,3},{3,2},{4,5},{5,4},{6,7},{7,6},{8,9},{9,8},{10,11... | collective-permute-start | bytes 1966088 | tf_op jit(solution)/shard_map/ppermute | solution.py:345
  3.4 12.4 %collective-permute-start = (f32[6,128,128]{2,1,0:T(8,128)S(1)}, f32[6,128,128]{2,1,0:T(8,128)S(1)}, u32[]{:S(2)}, u32[]{:S(2)}) collective-permute-start(f32[6,128,128]{2,1,0:T(8,128)S(1)} %get-tuple-element.26.own_a0.own_a.own_a1), channel_id=1, source_target_pairs={{1,2},{2,1},{3,4},{4,3},{5,6},{6,5},{7,8},{8,7},{9,10},{10,9},{11,... | collective-permute-start | bytes 1179656 | tf_op jit(solution)/shard_map/ppermute | solution.py:338
  9.9 11.0 %collective-permute-start.1 = (f32[4,128,128]{2,1,0:T(8,128)S(1)}, f32[4,128,128]{2,1,0:T(8,128)S(1)}, u32[]{:S(2)}, u32[]{:S(2)}) collective-permute-start(f32[4,128,128]{2,1,0:T(8,128)S(1)} %get-tuple-element.27.own_a.own_a1), channel_id=1, source_target_pairs={{1,2},{2,1},{3,4},{4,3},{5,6},{6,5},{7,8},{8,7},{9,10},{10,9},{11,... | collective-permute-start | bytes 786440 | tf_op jit(solution)/shard_map/ppermute | solution.py:338
  21.4 12.9 %collective-permute-start.4 = (f32[8,128,128]{2,1,0:T(8,128)S(1)}, f32[8,128,128]{2,1,0:T(8,128)S(1)}, u32[]{:S(2)}, u32[]{:S(2)}) collective-permute-start(f32[8,128,128]{2,1,0:T(8,128)S(1)} %get-tuple-element.32.own_b), channel_id=1, source_target_pairs={{0,1},{1,0},{2,3},{3,2},{4,5},{5,4},{6,7},{7,6},{8,9},{9,8},{10,11... | collective-permute-start | bytes 1572872 | tf_op jit(solution)/shard_map/ppermute | solution.py:345
  23.3 11.0 %collective-permute-start.5 = (f32[4,128,128]{2,1,0:T(8,128)S(1)}, f32[4,128,128]{2,1,0:T(8,128)S(1)}, u32[]{:S(2)}, u32[]{:S(2)}) collective-permute-start(f32[4,128,128]{2,1,0:T(8,128)S(1)} %get-tuple-element.33.own_a), channel_id=1, source_target_pairs={{1,2},{2,1},{3,4},{4,3},{5,6},{6,5},{7,8},{8,7},{9,10},{10,9},{11,... | collective-permute-start | bytes 786440 | tf_op jit(solution)/shard_map/ppermute | solution.py:338
  27.5 11.0 %collective-permute-start.3 = (f32[4,128,128]{2,1,0:T(8,128)S(1)}, f32[4,128,128]{2,1,0:T(8,128)S(1)}, u32[]{:S(2)}, u32[]{:S(2)}) collective-permute-start(f32[4,128,128]{2,1,0:T(8,128)S(1)} %get-tuple-element.31.own_a), channel_id=1, source_target_pairs={{1,2},{2,1},{3,4},{4,3},{5,6},{6,5},{7,8},{8,7},{9,10},{10,9},{11,... | collective-permute-start | bytes 786440 | tf_op jit(solution)/shard_map/ppermute | solution.py:338
  39.0 12.2 %collective-permute-start.7 = (f32[6,128,128]{2,1,0:T(8,128)S(1)}, f32[6,128,128]{2,1,0:T(8,128)S(1)}, u32[]{:S(2)}, u32[]{:S(2)}) collective-permute-start(f32[6,128,128]{2,1,0:T(8,128)S(1)} %get-tuple-element.36.own_b), channel_id=1, source_target_pairs={{0,1},{1,0},{2,3},{3,2},{4,5},{5,4},{6,7},{7,6},{8,9},{9,8},{10,11... | collective-permute-start | bytes 1179656 | tf_op jit(solution)/shard_map/ppermute | solution.py:345
  41.0 10.3 %collective-permute-start.8 = (f32[3,128,128]{2,1,0:T(8,128)S(1)}, f32[3,128,128]{2,1,0:T(8,128)S(1)}, u32[]{:S(2)}, u32[]{:S(2)}) collective-permute-start(f32[3,128,128]{2,1,0:T(8,128)S(1)} %get-tuple-element.40.own_a), channel_id=1, source_target_pairs={{1,2},{2,1},{3,4},{4,3},{5,6},{6,5},{7,8},{8,7},{9,10},{10,9},{11,... | collective-permute-start | bytes 589832 | tf_op jit(solution)/shard_map/ppermute | solution.py:338
  45.6 10.3 %collective-permute-start.6 = (f32[3,128,128]{2,1,0:T(8,128)S(1)}, f32[3,128,128]{2,1,0:T(8,128)S(1)}, u32[]{:S(2)}, u32[]{:S(2)}) collective-permute-start(f32[3,128,128]{2,1,0:T(8,128)S(1)} %get-tuple-element.35.own_a), channel_id=1, source_target_pairs={{1,2},{2,1},{3,4},{4,3},{5,6},{6,5},{7,8},{8,7},{9,10},{10,9},{11,... | collective-permute-start | bytes 589832 | tf_op jit(solution)/shard_map/ppermute | solution.py:338
  67.2 14.5 %collective-permute-start.9 = (f32[2,2,16,128]{3,2,1,0:T(8,128)S(1)}, f32[2,2,16,128]{3,2,1,0:T(8,128)S(1)}, u32[]{:S(2)}, u32[]{:S(2)}) collective-permute-start(f32[2,2,16,128]{3,2,1,0:T(8,128)S(1)} %get-tuple-element.44), channel_id=1, source_target_pairs={{0,64},{64,0},{128,192},{192,128},{256,320},{320,256},{384,448},{4... | collective-permute-start | bytes 98312 | tf_op jit(solution)/shard_map/ppermute | solution.py:369

commit v4 on v3

--- a/solution.py
+++ b/solution.py
@@ -85,19 +85,20 @@
     return jnp.where((at == 0) | (at == last), 0.0, 1.0).astype(jnp.float32)
 
 
-def probe_at(parts, p):
-    ref, at = parts[p]
-    return (ref, at + 2) if p == 0 else (ref, at)
-
-
-def first_of(parts, p, r, n):
-    (gain, gain_at), (ref, at) = parts[0], probe_at(parts, p)
-    return scale(ref[at, r : r + n], load(gain, gain_at, r, n))
+def first_of(layer, parts, p, r, n):
+    if layer == 0:
+        return load(parts[p], 0, r, n)
+    both = parts[2]
+    return scale(both[2 + 4 * p, r : r + n], load(both, 0, r, n))
+
+
+def partial_of(layer, parts, p, r, n):
+    return load(parts[p], 2, r, n) if layer == 0 else load(parts[2], 3 + 4 * p, r, n)
 
 
 def start_kernel(
     shifts_hbm, back_hbm, probes_hbm, medium_hbm, receivers_hbm,
-    out_a0, out_a1, out_b, inv, waves, row,
+    out_a0, out_a1, out_b, later, inv, waves, row,
     shifts, back, probes, medium, receivers, pad, sems,
 ):
     copies = [
@@ -117,7 +118,9 @@
     near = side()
     own = (near, 1 - near)
     height = medium.shape[1]
-    outs = ((out_a0, 0), (out_a1, 0)), ((out_b, 0), (out_b, 6))
+    medium_at = ((out_a0, 4), (out_b, 5))
+    gain_at = ((later, 0), (out_b, 0))
+    heard_at = ((later, 2), (out_b, 9))
     clear_edges(pad)
     copies[0].wait()
     shift_re, shift_im = shifts[0, 0], shifts[0, 1]
@@ -125,13 +128,14 @@
     row[1] = jnp.full(row.shape[1:], shift_im, jnp.float32)
     copies[1].wait()
     for layer in range(2):
+        ref, at = medium_at[layer]
         for r, n in chunks(height):
             med = medium[own[layer], r : r + n]
             store(inv, 2 * layer, r, n, inverse(med, shift_re, shift_im))
-            outs[layer][0][0][outs[layer][0][1] + 5, r : r + n] = med
+            ref[at, r : r + n] = med
     copies[2].wait()
     for layer in range(2):
-        ref, at = outs[layer][0]
+        ref, at = gain_at[layer]
         for r, n in chunks(height):
             rows = slice(r, r + n)
             bg = (back[0, 0, own[layer], rows], back[0, 1, own[layer], rows])
@@ -140,25 +144,29 @@
             store(ref, at, r, n, multiply(load(inv, 2 * layer, r, n), wave))
     copies[3].wait()
     for p in range(2):
+        link = (out_a0, out_a1)[p]
         for layer in range(2):
-            gain, gain_at = outs[layer][0]
-            ref, at = probe_at(outs[layer], p)
+            gain, at = gain_at[layer]
             for r, n in chunks(height):
                 probe = probes[p, own[layer], r : r + n]
-                ref[at, r : r + n] = probe
-                store(pad, 2 * layer, TOP + r, n, scale(probe, load(gain, gain_at, r, n)))
+                first = scale(probe, load(gain, at, r, n))
+                store(pad, 2 * layer, TOP + r, n, first)
+                if layer == 0:
+                    store(link, 0, r, n, first)
+                else:
+                    out_b[2 + 4 * p, r : r + n] = probe
         for layer in range(2):
-            ref, at = probe_at(outs[layer], p)
+            ref, at = ((link, 2), (out_b, 3 + 4 * p))[layer]
             for r, n in chunks(height):
                 here, around = complex_in_plane(pad, layer, r, n)
                 around = add(around, load(pad, 2 * (1 - layer), TOP + r, n))
                 part = add(scale(1.0 + KEEP, here), multiply(load(inv, 2 * layer, r, n), around))
-                store(ref, at + 1, r, n, part)
+                store(ref, at, r, n, part)
     copies[4].wait()
     for layer in range(2):
-        ref, at = outs[layer][1]
-        for r, n in chunks(height):
-            ref[at + 3, r : r + n] = receivers[own[layer], r : r + n].astype(jnp.float32)
+        ref, at = heard_at[layer]
+        for r, n in chunks(height):
+            ref[at, r : r + n] = receivers[own[layer], r : r + n].astype(jnp.float32)
 
 
 def halo_inverse(med, layer, row, mask):
@@ -166,36 +174,39 @@
     return (mask * re, mask * im) if layer == 0 else (re, im)
 
 
-def forward_kernel(p, row, own_a0, own_a, own_b, got_a0, got_a, got_b, inv, *rest):
+def forward_kernel(
+    p, row, own_a0, own_a1, own_b, got_a0, got_a1, got_b, inv, extra, *rest
+):
+    height = inv.shape[1]
     if p == 0:
         out_a, out_b, pad, spare = rest
         out_at = 0
+        for k in range(extra.shape[0]):
+            for r, n in chunks(height):
+                out_a[4 + k, r : r + n] = extra[k, r : r + n]
     else:
-        first_b, out_a, out_b, pad, spare = rest
+        out_a, out_b, pad, spare = rest
         out_at = 4
-        out_b[0:4] = first_b[...]
+        out_b[0:4] = extra[...]
     mask = has_partner()
-    height = inv.shape[1]
-    own = ((own_a0, 0), (own_a, 0)), ((own_b, 0), (own_b, 6))
-    got = ((got_a0, 0), (got_a, 0)), ((got_b, 0), (got_b, 6))
+    own = (own_a0, own_a1, own_b)
+    got = (got_a0, got_a1, got_b)
+    med = ((got_a0, 4), (got_b, 5))
     out = ((out_a, 0), (out_b, out_at))
     clear_edges(pad)
     clear_edges(spare)
     for layer in range(2):
-        mine, at = probe_at(own[layer], p)
         for r, n in chunks(height):
             second = add(
-                load(mine, at + 1, r, n),
-                multiply(load(inv, 2 * layer, r, n), first_of(got[layer], p, r, n)),
+                partial_of(layer, own, p, r, n),
+                multiply(load(inv, 2 * layer, r, n), first_of(layer, got, p, r, n)),
             )
             store(pad, 2 * layer, TOP + r, n, second)
     for layer in range(2):
-        theirs, from_ = probe_at(got[layer], p)
-        med, med_at = got[layer][0]
-        for r, n in chunks(height):
-            first = first_of(own[layer], p, r, n)
-            there = halo_inverse(med[med_at + 5, r : r + n], layer, row, mask)
-            halo = add(load(theirs, from_ + 1, r, n), multiply(there, first))
+        for r, n in chunks(height):
+            first = first_of(layer, own, p, r, n)
+            there = halo_inverse(med[layer][0][med[layer][1], r : r + n], layer, row, mask)
+            halo = add(partial_of(layer, got, p, r, n), multiply(there, first))
             here, around = complex_in_plane(pad, layer, r, n)
             around = add(add(around, halo), load(pad, 2 * (1 - layer), TOP + r, n))
             third = add(
@@ -208,14 +219,14 @@
             here, around = complex_in_plane(spare, layer, r, n)
             around = add(around, load(spare, 2 * (1 - layer), TOP + r, n))
             part = add(
-                add(scale(KEEP, here), first_of(own[layer], p, r, n)),
+                add(scale(KEEP, here), first_of(layer, own, p, r, n)),
                 multiply(load(inv, 2 * layer, r, n), around),
             )
             store(out[layer][0], out[layer][1] + 2, r, n, part)
 
 
 def turn_kernel(
-    p, row, own_a, own_b, got_a, got_b, med_a, got_b1, rec_a, own_a1, own_b1, inv, *rest
+    p, row, own_a, own_b, got_a, got_b, med_a, got_a2, got_b1, later, own_b1, inv, *rest
 ):
     if p == 0:
         out_a, out_b, right, part_sum, pad, spare = rest
@@ -228,10 +239,10 @@
     height = inv.shape[1]
     own = ((own_a, 0), (own_b, 0 if p == 0 else b_at))
     got = ((got_a, 0), (got_b, b_at))
-    med = ((med_a, 5), (got_b1, 5))
-    rec_own = ((own_a1, 3), (own_b1, 9))
-    rec_got = ((rec_a, 3), (got_b1, 9))
-    gain = (med_a, got_b1)
+    med = ((med_a, 4), (got_b1, 5))
+    rec_own = ((later, 2), (own_b1, 9))
+    rec_got = ((got_a2, 6), (got_b1, 9))
+    gain = ((got_a2, 4), (got_b1, 0))
     out = ((out_a, 0), (out_b, out_at))
     clear_edges(pad)
     clear_edges(spare)
@@ -268,11 +279,11 @@
                 multiply_conj(load(inv, 2 * layer, r, n), around),
             )
             store(part_sum, 2 * layer, r, n, part)
-            seen = load(gain[layer], 0, r, n)
+            seen = load(*gain[layer], r, n)
             out[layer][0][out[layer][1] + 2, r : r + n] = seen[0] * part[0] + seen[1] * part[1]
 
 
-def end_kernel(p, row, own_a, own_b, got_a, got_b, med_a, got_b1, inv, right, part_sum, waves, own_a1, own_b1, *rest):
+def end_kernel(p, row, own_a, own_b, got_a, got_b, med_a, got_b1, inv, right, part_sum, waves, later, own_b1, *rest):
     if p == 0:
         out, pad = rest
         b_at, out_at = 0, 0
@@ -287,8 +298,8 @@
     strip = out.shape[3]
     own = ((own_a, 0), (own_b, 0 if p == 0 else b_at))
     got = ((got_a, 0), (got_b, b_at))
-    med = ((med_a, 5), (got_b1, 5))
-    gain = (own_a1, own_b1)
+    med = ((med_a, 4), (got_b1, 5))
+    gain = (later, own_b1)
     clear_edges(pad)
     for layer in range(2):
         (mine, at), (theirs, from_) = own[layer], got[layer]
@@ -372,13 +383,13 @@
 def per_device(probes, background, medium, shifts, receivers):
     plane = medium.shape[1:]
     pad = pltpu.VMEM((4, plane[0] + 2 * TOP, plane[1]), jnp.float32)
-    three, four, six, eight, ten = [(k, *plane) for k in (3, 4, 6, 8, 10)]
+    three, four, five, six, seven, eight, ten = [(k, *plane) for k in (3, 4, 5, 6, 7, 8, 10)]
     args = (shifts, background, probes, medium, receivers)
     held = [pltpu.VMEM(v.shape, v.dtype) for v in args[1:]]
     a1 = [None, None]
-    a1[0], a1[1], b1, inv, waves, row = call(
+    a1[0], a1[1], b1, later, inv, waves, row = call(
         start_kernel,
-        [six, four, ten, four, four, (2, 8, plane[1])],
+        [five, four, ten, three, four, four, (2, 8, plane[1])],
         [pltpu.SMEM(shifts.shape, shifts.dtype), *held, pad, pltpu.SemaphoreType.DMA((5,))],
         *[pltpu.with_memory_space_constraint(v, pltpu.HBM) for v in args],
         space=pltpu.HBM,
@@ -389,9 +400,9 @@
     for p in range(2):
         a2[p], out_b = call(
             functools.partial(forward_kernel, p),
-            [four, eight if p else four],
+            [four, eight] if p else [seven, four],
             [pad, pad],
-            row, a1[0], a1[p], b1, ra1[0], ra1[p], rb1, inv, *b2,
+            row, a1[0], a1[p], b1, ra1[0], ra1[p], rb1, inv, b2[0] if p else later,
         )
         b2.append(out_b)
         ra2[p] = swap_links(a2[p])
@@ -403,7 +414,7 @@
             functools.partial(turn_kernel, p),
             [three, six if p else three, four, four],
             [pad, pad],
-            row, a2[p], b2[p], ra2[p], rb2, ra1[0], rb1, ra1[1], a1[1], b1, inv, *b3,
+            row, a2[p], b2[p], ra2[p], rb2, ra1[0], ra2[0], rb1, later, b1, inv, *b3,
         )
         b3.append(out_b)
         ra3[p] = swap_links(a3[p])
@@ -416,7 +427,7 @@
             [(blocks, p + 1, 2, plane[0] // blocks, plane[1])],
             [pad],
             row, a3[p], b3[p], ra3[p], rb3, ra1[0], rb1, inv, right[p], part_sum[p],
-            waves, a1[0], b1, *terms,
+            waves, later, b1, *terms,
         )
         terms.append(out)
     return reduced(terms[1])

time: 82.8 us -> 82.8 us (level)
  no operation moved by 1% of the time
where the time goes in v4:
time: 82.8 us; the launch traced here: 82.4 us
  starting transfers between devices  34.5 us (42%)
  waiting for transfers between devices  32.1 us (39%)
  blocking collectives  10.9 us (13%)
  Pallas kernels  4.11 us (5%)
    ppermute x6, starting transfers between devices, swap_links(): return lax.ppermute(x, 'space', pairs)  26.6 us
    ppermute x6, waiting for transfers between devices, swap_links(): return lax.ppermute(x, 'space', pairs)  19.7 us
    ppermute x1, waiting for transfers between devices, reduced(): return keep + lax.ppermute(send, 'freq', pairs)  12.4 us
    all_to_all x1, blocking collectives, reduced(): lax.all_to_all(terms, 'freq', split_axis=0, concat_axis=0, axis_index_gro...  10.9 us
    ppermute x3, starting transfers between devices, swap_cores(): return lax.ppermute(x, 'space', pairs)  5.76 us
    pallas_call x8, Pallas kernels, call(): pl.pallas_call(kernel, out_shape=[jax.ShapeDtypeStruct(s, jnp.float32) fo...  4.11 us
    ppermute x1, starting transfers between devices, reduced(): return keep + lax.ppermute(send, 'freq', pairs)  2.12 us
  transfers between devices with their start and end apart: 10, of which 7 were waited for; matrix products, arithmetic and copies ran while one was open for 0% of the time, Pallas kernels for 2%

profile of v4, /device:TPU:384, one launch (start us, length us, event | category | flops | bytes accessed | tf_op | source)
XLA Modules:
  0.0 82.4 jit_solution(10508039822294700696)
XLA Ops:
  0.0 1.5 %shard_map.55 = (f32[5,128,128]{2,1,0:T(8,128)S(1)}, f32[4,128,128]{2,1,0:T(8,128)S(1)}, f32[10,128,128]{2,1,0:T(8,128)S(1)}, f32[3,128,128]{2,1,0:T(8,128)S(1)}...) custom-call(f32[1,2]{1,0:T(1,128)} %shifts_hbm.1, ...), custom_call_target="tpu_custom_call" | custom-call | flops 2000000 | bytes 2000000 | tf_op jit(solution)/shard_map/pallas_call | solution.py:333
  1.5 1.9 %collective-permute-start.2 = (f32[10,128,128]{2,1,0:T(8,128)S(1)}, f32[10,128,128]{2,1,0:T(8,128)S(1)}, u32[]{:S(2)}, u32[]{:S(2)}) collective-permute-start(f32[10,128,128]{2,1,0:T(8,128)S(1)} %get-tuple-element.29.own_b.own_b1), channel_id=1, source_target_pairs={{0,1},{1,0},{2,3},{3,2},{4,5},{5,4},{6,7},{7,6},{8,9},{9,8},{10,11... | collective-permute-start | bytes 1966088 | tf_op jit(solution)/shard_map/ppermute | solution.py:356
  3.5 6.4 %collective-permute-start = (f32[5,128,128]{2,1,0:T(8,128)S(1)}, f32[5,128,128]{2,1,0:T(8,128)S(1)}, u32[]{:S(2)}, u32[]{:S(2)}) collective-permute-start(f32[5,128,128]{2,1,0:T(8,128)S(1)} %get-tuple-element.27.own_a0.own_a1), channel_id=1, source_target_pairs={{1,2},{2,1},{3,4},{4,3},{5,6},{6,5},{7,8},{8,7},{9,10},{10,9},{11,... | collective-permute-start | bytes 983048 | tf_op jit(solution)/shard_map/ppermute | solution.py:349
  9.9 2.5 %collective-permute-start.1 = (f32[4,128,128]{2,1,0:T(8,128)S(1)}, f32[4,128,128]{2,1,0:T(8,128)S(1)}, u32[]{:S(2)}, u32[]{:S(2)}) collective-permute-start(f32[4,128,128]{2,1,0:T(8,128)S(1)} %get-tuple-element.28.own_a1), channel_id=1, source_target_pairs={{1,2},{2,1},{3,4},{4,3},{5,6},{6,5},{7,8},{8,7},{9,10},{10,9},{11,... | collective-permute-start | bytes 786440 | tf_op jit(solution)/shard_map/ppermute | solution.py:349
  12.4 2.8 %collective-permute-done.got_a0.got_a1.med_a = f32[5,128,128]{2,1,0:T(8,128)S(1)} collective-permute-done((f32[5,128,128]{2,1,0:T(8,128)S(1)}, f32[5,128,128]{2,1,0:T(8,128)S(1)}, u32[]{:S(2)}, u32[]{:S(2)}) %collective-permute-start) | collective-permute-done | bytes 327712 | tf_op jit(solution)/shard_map/ppermute | solution.py:349
  15.2 0.5 shard_map.56
  15.7 5.3 %collective-permute-done.1.got_a1 = f32[4,128,128]{2,1,0:T(8,128)S(1)} collective-permute-done((f32[4,128,128]{2,1,0:T(8,128)S(1)}, f32[4,128,128]{2,1,0:T(8,128)S(1)}, u32[]{:S(2)}, u32[]{:S(2)}) %collective-permute-start.1) | collective-permute-done | bytes 262176 | tf_op jit(solution)/shard_map/ppermute | solution.py:349
  20.9 0.5 shard_map.57
  21.4 1.9 %collective-permute-start.4 = (f32[8,128,128]{2,1,0:T(8,128)S(1)}, f32[8,128,128]{2,1,0:T(8,128)S(1)}, u32[]{:S(2)}, u32[]{:S(2)}) collective-permute-start(f32[8,128,128]{2,1,0:T(8,128)S(1)} %get-tuple-element.34.own_b), channel_id=1, source_target_pairs={{0,1},{1,0},{2,3},{3,2},{4,5},{5,4},{6,7},{7,6},{8,9},{9,8},{10,11... | collective-permute-start | bytes 1572872 | tf_op jit(solution)/shard_map/ppermute | solution.py:356
  23.3 3.5 %collective-permute-start.5 = (f32[7,128,128]{2,1,0:T(8,128)S(1)}, f32[7,128,128]{2,1,0:T(8,128)S(1)}, u32[]{:S(2)}, u32[]{:S(2)}) collective-permute-start(f32[7,128,128]{2,1,0:T(8,128)S(1)} %get-tuple-element.35.own_a), channel_id=1, source_target_pairs={{1,2},{2,1},{3,4},{4,3},{5,6},{6,5},{7,8},{8,7},{9,10},{10,9},{11,... | collective-permute-start | bytes 1376264 | tf_op jit(solution)/shard_map/ppermute | solution.py:349
  26.8 5.4 %collective-permute-start.3 = (f32[4,128,128]{2,1,0:T(8,128)S(1)}, f32[4,128,128]{2,1,0:T(8,128)S(1)}, u32[]{:S(2)}, u32[]{:S(2)}) collective-permute-start(f32[4,128,128]{2,1,0:T(8,128)S(1)} %get-tuple-element.33.own_a), channel_id=1, source_target_pairs={{1,2},{2,1},{3,4},{4,3},{5,6},{6,5},{7,8},{8,7},{9,10},{10,9},{11,... | collective-permute-start | bytes 786440 | tf_op jit(solution)/shard_map/ppermute | solution.py:349
  32.2 4.2 %collective-permute-done.5.got_a.got_a2 = f32[7,128,128]{2,1,0:T(8,128)S(1)} collective-permute-done((f32[7,128,128]{2,1,0:T(8,128)S(1)}, f32[7,128,128]{2,1,0:T(8,128)S(1)}, u32[]{:S(2)}, u32[]{:S(2)}) %collective-permute-start.5) | collective-permute-done | bytes 458784 | tf_op jit(solution)/shard_map/ppermute | solution.py:349
  36.4 0.5 shard_map.58
  36.9 2.3 %collective-permute-done.3.got_a = f32[4,128,128]{2,1,0:T(8,128)S(1)} collective-permute-done((f32[4,128,128]{2,1,0:T(8,128)S(1)}, f32[4,128,128]{2,1,0:T(8,128)S(1)}, u32[]{:S(2)}, u32[]{:S(2)}) %collective-permute-start.3) | collective-permute-done | bytes 262176 | tf_op jit(solution)/shard_map/ppermute | solution.py:349
  39.2 0.5 shard_map.59
  39.8 1.9 %collective-permute-start.7 = (f32[6,128,128]{2,1,0:T(8,128)S(1)}, f32[6,128,128]{2,1,0:T(8,128)S(1)}, u32[]{:S(2)}, u32[]{:S(2)}) collective-permute-start(f32[6,128,128]{2,1,0:T(8,128)S(1)} %get-tuple-element.38.own_b), channel_id=1, source_target_pairs={{0,1},{1,0},{2,3},{3,2},{4,5},{5,4},{6,7},{7,6},{8,9},{9,8},{10,11... | collective-permute-start | bytes 1179656 | tf_op jit(solution)/shard_map/ppermute | solution.py:356
  41.7 4.0 %collective-permute-start.8 = (f32[3,128,128]{2,1,0:T(8,128)S(1)}, f32[3,128,128]{2,1,0:T(8,128)S(1)}, u32[]{:S(2)}, u32[]{:S(2)}) collective-permute-start(f32[3,128,128]{2,1,0:T(8,128)S(1)} %get-tuple-element.42.own_a), channel_id=1, source_target_pairs={{1,2},{2,1},{3,4},{4,3},{5,6},{6,5},{7,8},{8,7},{9,10},{10,9},{11,... | collective-permute-start | bytes 589832 | tf_op jit(solution)/shard_map/ppermute | solution.py:349
  45.7 4.9 %collective-permute-start.6 = (f32[3,128,128]{2,1,0:T(8,128)S(1)}, f32[3,128,128]{2,1,0:T(8,128)S(1)}, u32[]{:S(2)}, u32[]{:S(2)}) collective-permute-start(f32[3,128,128]{2,1,0:T(8,128)S(1)} %get-tuple-element.37.own_a), channel_id=1, source_target_pairs={{1,2},{2,1},{3,4},{4,3},{5,6},{6,5},{7,8},{8,7},{9,10},{10,9},{11,... | collective-permute-start | bytes 589832 | tf_op jit(solution)/shard_map/ppermute | solution.py:349
  50.6 1.4 %collective-permute-done.8.got_a = f32[3,128,128]{2,1,0:T(8,128)S(1)} collective-permute-done((f32[3,128,128]{2,1,0:T(8,128)S(1)}, f32[3,128,128]{2,1,0:T(8,128)S(1)}, u32[]{:S(2)}, u32[]{:S(2)}) %collective-permute-start.8) | collective-permute-done | bytes 196640 | tf_op jit(solution)/shard_map/ppermute | solution.py:349
  52.3 3.7 %collective-permute-done.6.got_a = f32[3,128,128]{2,1,0:T(8,128)S(1)} collective-permute-done((f32[3,128,128]{2,1,0:T(8,128)S(1)}, f32[3,128,128]{2,1,0:T(8,128)S(1)}, u32[]{:S(2)}, u32[]{:S(2)}) %collective-permute-start.6) | collective-permute-done | bytes 196640 | tf_op jit(solution)/shard_map/ppermute | solution.py:349
  56.3 10.9 %all_to_all.5.arrived = f32[8,2,2,16,128]{4,3,2,1,0:T(8,128)S(1)} all-to-all(f32[8,2,2,16,128]{4,3,2,1,0:T(8,128)S(1)} %shard_map.61), channel_id=1, replica_groups={{0,128,256,384},{64,192,320,448},{1,129,257,385},{65,193,321,449},{2,13..., dimensions={0} | all-to-all | bytes 524288 | tf_op jit(solution)/shard_map/all_to_all | solution.py:374
  67.3 2.1 %collective-permute-start.9 = (f32[2,2,16,128]{3,2,1,0:T(8,128)S(1)}, f32[2,2,16,128]{3,2,1,0:T(8,128)S(1)}, u32[]{:S(2)}, u32[]{:S(2)}) collective-permute-start(f32[2,2,16,128]{3,2,1,0:T(8,128)S(1)} %get-tuple-element.46), channel_id=1, source_target_pairs={{0,64},{64,0},{128,192},{192,128},{256,320},{320,256},{384,448},{4... | collective-permute-start | bytes 98312 | tf_op jit(solution)/shard_map/ppermute | solution.py:380
  69.4 12.4 %collective-permute-done.9 = f32[2,2,16,128]{3,2,1,0:T(8,128)S(1)} collective-permute-done((f32[2,2,16,128]{3,2,1,0:T(8,128)S(1)}, f32[2,2,16,128]{3,2,1,0:T(8,128)S(1)}, u32[]{:S(2)}, u32[]{:S(2)}) %collective-permute-start.9) | collective-permute-done | bytes 32800 | tf_op jit(solution)/shard_map/ppermute | solution.py:380
  81.8 0.6 add.3
  (6 shorter events, 0.6 us)
Async XLA Ops:
  1.5 13.6 %collective-permute-start.2 = (f32[10,128,128]{2,1,0:T(8,128)S(1)}, f32[10,128,128]{2,1,0:T(8,128)S(1)}, u32[]{:S(2)}, u32[]{:S(2)}) collective-permute-start(f32[10,128,128]{2,1,0:T(8,128)S(1)} %get-tuple-element.29.own_b.own_b1), channel_id=1, source_target_pairs={{0,1},{1,0},{2,3},{3,2},{4,5},{5,4},{6,7},{7,6},{8,9},{9,8},{10,11... | collective-permute-start | bytes 1966088 | tf_op jit(solution)/shard_map/ppermute | solution.py:356
  3.5 11.7 %collective-permute-start = (f32[5,128,128]{2,1,0:T(8,128)S(1)}, f32[5,128,128]{2,1,0:T(8,128)S(1)}, u32[]{:S(2)}, u32[]{:S(2)}) collective-permute-start(f32[5,128,128]{2,1,0:T(8,128)S(1)} %get-tuple-element.27.own_a0.own_a1), channel_id=1, source_target_pairs={{1,2},{2,1},{3,4},{4,3},{5,6},{6,5},{7,8},{8,7},{9,10},{10,9},{11,... | collective-permute-start | bytes 983048 | tf_op jit(solution)/shard_map/ppermute | solution.py:349
  9.9 11.0 %collective-permute-start.1 = (f32[4,128,128]{2,1,0:T(8,128)S(1)}, f32[4,128,128]{2,1,0:T(8,128)S(1)}, u32[]{:S(2)}, u32[]{:S(2)}) collective-permute-start(f32[4,128,128]{2,1,0:T(8,128)S(1)} %get-tuple-element.28.own_a1), channel_id=1, source_target_pairs={{1,2},{2,1},{3,4},{4,3},{5,6},{6,5},{7,8},{8,7},{9,10},{10,9},{11,... | collective-permute-start | bytes 786440 | tf_op jit(solution)/shard_map/ppermute | solution.py:349
  21.4 15.0 %collective-permute-start.4 = (f32[8,128,128]{2,1,0:T(8,128)S(1)}, f32[8,128,128]{2,1,0:T(8,128)S(1)}, u32[]{:S(2)}, u32[]{:S(2)}) collective-permute-start(f32[8,128,128]{2,1,0:T(8,128)S(1)} %get-tuple-element.34.own_b), channel_id=1, source_target_pairs={{0,1},{1,0},{2,3},{3,2},{4,5},{5,4},{6,7},{7,6},{8,9},{9,8},{10,11... | collective-permute-start | bytes 1572872 | tf_op jit(solution)/shard_map/ppermute | solution.py:356
  23.3 13.1 %collective-permute-start.5 = (f32[7,128,128]{2,1,0:T(8,128)S(1)}, f32[7,128,128]{2,1,0:T(8,128)S(1)}, u32[]{:S(2)}, u32[]{:S(2)}) collective-permute-start(f32[7,128,128]{2,1,0:T(8,128)S(1)} %get-tuple-element.35.own_a), channel_id=1, source_target_pairs={{1,2},{2,1},{3,4},{4,3},{5,6},{6,5},{7,8},{8,7},{9,10},{10,9},{11,... | collective-permute-start | bytes 1376264 | tf_op jit(solution)/shard_map/ppermute | solution.py:349
  26.8 12.4 %collective-permute-start.3 = (f32[4,128,128]{2,1,0:T(8,128)S(1)}, f32[4,128,128]{2,1,0:T(8,128)S(1)}, u32[]{:S(2)}, u32[]{:S(2)}) collective-permute-start(f32[4,128,128]{2,1,0:T(8,128)S(1)} %get-tuple-element.33.own_a), channel_id=1, source_target_pairs={{1,2},{2,1},{3,4},{4,3},{5,6},{6,5},{7,8},{8,7},{9,10},{10,9},{11,... | collective-permute-start | bytes 786440 | tf_op jit(solution)/shard_map/ppermute | solution.py:349
  39.8 12.2 %collective-permute-start.7 = (f32[6,128,128]{2,1,0:T(8,128)S(1)}, f32[6,128,128]{2,1,0:T(8,128)S(1)}, u32[]{:S(2)}, u32[]{:S(2)}) collective-permute-start(f32[6,128,128]{2,1,0:T(8,128)S(1)} %get-tuple-element.38.own_b), channel_id=1, source_target_pairs={{0,1},{1,0},{2,3},{3,2},{4,5},{5,4},{6,7},{7,6},{8,9},{9,8},{10,11... | collective-permute-start | bytes 1179656 | tf_op jit(solution)/shard_map/ppermute | solution.py:356
  41.7 10.3 %collective-permute-start.8 = (f32[3,128,128]{2,1,0:T(8,128)S(1)}, f32[3,128,128]{2,1,0:T(8,128)S(1)}, u32[]{:S(2)}, u32[]{:S(2)}) collective-permute-start(f32[3,128,128]{2,1,0:T(8,128)S(1)} %get-tuple-element.42.own_a), channel_id=1, source_target_pairs={{1,2},{2,1},{3,4},{4,3},{5,6},{6,5},{7,8},{8,7},{9,10},{10,9},{11,... | collective-permute-start | bytes 589832 | tf_op jit(solution)/shard_map/ppermute | solution.py:349
  45.7 10.3 %collective-permute-start.6 = (f32[3,128,128]{2,1,0:T(8,128)S(1)}, f32[3,128,128]{2,1,0:T(8,128)S(1)}, u32[]{:S(2)}, u32[]{:S(2)}) collective-permute-start(f32[3,128,128]{2,1,0:T(8,128)S(1)} %get-tuple-element.37.own_a), channel_id=1, source_target_pairs={{1,2},{2,1},{3,4},{4,3},{5,6},{6,5},{7,8},{8,7},{9,10},{10,9},{11,... | collective-permute-start | bytes 589832 | tf_op jit(solution)/shard_map/ppermute | solution.py:349
  67.3 14.5 %collective-permute-start.9 = (f32[2,2,16,128]{3,2,1,0:T(8,128)S(1)}, f32[2,2,16,128]{3,2,1,0:T(8,128)S(1)}, u32[]{:S(2)}, u32[]{:S(2)}) collective-permute-start(f32[2,2,16,128]{3,2,1,0:T(8,128)S(1)} %get-tuple-element.46), channel_id=1, source_target_pairs={{0,64},{64,0},{128,192},{192,128},{256,320},{320,256},{384,448},{4... | collective-permute-start | bytes 98312 | tf_op jit(solution)/shard_map/ppermute | solution.py:380

commit v5 on v4

--- a/solution.py
+++ b/solution.py
@@ -232,8 +232,9 @@
         out_a, out_b, right, part_sum, pad, spare = rest
         b_at, out_at = 0, 0
     else:
-        first_b, out_a, out_b, right, part_sum, pad, spare = rest
+        first_a, first_b, out_a, out_b, right, part_sum, pad, spare = rest
         b_at, out_at = 4, 3
+        out_a[0:3] = first_a[...]
         out_b[0:3] = first_b[...]
     mask = has_partner()
     height = inv.shape[1]
@@ -243,7 +244,7 @@
     rec_own = ((later, 2), (own_b1, 9))
     rec_got = ((got_a2, 6), (got_b1, 9))
     gain = ((got_a2, 4), (got_b1, 0))
-    out = ((out_a, 0), (out_b, out_at))
+    out = ((out_a, out_at), (out_b, out_at))
     clear_edges(pad)
     clear_edges(spare)
     for layer in range(2):
@@ -296,8 +297,8 @@
     place = (near, 1 - near)
     height = inv.shape[1]
     strip = out.shape[3]
-    own = ((own_a, 0), (own_b, 0 if p == 0 else b_at))
-    got = ((got_a, 0), (got_b, b_at))
+    own = ((own_a, b_at), (own_b, b_at))
+    got = ((got_a, b_at), (got_b, b_at))
     med = ((med_a, 4), (got_b1, 5))
     gain = (later, own_b1)
     clear_edges(pad)
@@ -407,17 +408,18 @@
         b2.append(out_b)
         ra2[p] = swap_links(a2[p])
     rb2 = swap_cores(b2[1])
-    a3, ra3, b3 = [None, None], [None, None], []
+    a3, b3 = [], []
     right, part_sum = [None, None], [None, None]
     for p in range(2):
-        a3[p], out_b, right[p], part_sum[p] = call(
+        out_a, out_b, right[p], part_sum[p] = call(
             functools.partial(turn_kernel, p),
-            [three, six if p else three, four, four],
+            [six if p else three] * 2 + [four, four],
             [pad, pad],
-            row, a2[p], b2[p], ra2[p], rb2, ra1[0], ra2[0], rb1, later, b1, inv, *b3,
+            row, a2[p], b2[p], ra2[p], rb2, ra1[0], ra2[0], rb1, later, b1, inv, *a3, *b3,
         )
+        a3.append(out_a)
         b3.append(out_b)
-        ra3[p] = swap_links(a3[p])
+    ra3 = swap_links(a3[1])
     rb3 = swap_cores(b3[1])
     blocks = lax.axis_size("freq")
     terms = []
@@ -426,7 +428,7 @@
             functools.partial(end_kernel, p),
             [(blocks, p + 1, 2, plane[0] // blocks, plane[1])],
             [pad],
-            row, a3[p], b3[p], ra3[p], rb3, ra1[0], rb1, inv, right[p], part_sum[p],
+            row, a3[p], b3[p], ra3, rb3, ra1[0], rb1, inv, right[p], part_sum[p],
             waves, later, b1, *terms,
         )
         terms.append(out)

time: 82.8 us -> 79.4 us (0.959)
  starting transfers between devices: 34.5 us -> 29.4 us
  waiting for transfers between devices: 32.1 us -> 33.7 us
    ppermute x6 -> x5, starting transfers between devices: 26.6 us -> 21.7 us  [swap_links(): return lax.ppermute(x, 'space', pairs)]
    ppermute x6 -> x5, waiting for transfers between devices: 19.7 us -> 21.1 us  [swap_links(): return lax.ppermute(x, 'space', pairs)]
  transfers between devices with their start and end apart: 10 -> 9, of which waited for: 7 -> 6; matrix products, arithmetic and copies ran while one was open for 0% -> 0% of each run, Pallas kernels for 2% -> 1%
where the time goes in v5:
time: 79.4 us; the launch traced here: 78.9 us
  waiting for transfers between devices  33.7 us (42%)
  starting transfers between devices  29.4 us (37%)
  blocking collectives  10.9 us (14%)
  Pallas kernels  4.14 us (5%)
    ppermute x5, starting transfers between devices, swap_links(): return lax.ppermute(x, 'space', pairs)  21.7 us
    ppermute x5, waiting for transfers between devices, swap_links(): return lax.ppermute(x, 'space', pairs)  21.1 us
    ppermute x1, waiting for transfers between devices, reduced(): return keep + lax.ppermute(send, 'freq', pairs)  12.6 us
    all_to_all x1, blocking collectives, reduced(): lax.all_to_all(terms, 'freq', split_axis=0, concat_axis=0, axis_index_gro...  10.9 us
    ppermute x3, starting transfers between devices, swap_cores(): return lax.ppermute(x, 'space', pairs)  5.76 us
    pallas_call x8, Pallas kernels, call(): pl.pallas_call(kernel, out_shape=[jax.ShapeDtypeStruct(s, jnp.float32) fo...  4.14 us
    ppermute x1, starting transfers between devices, reduced(): return keep + lax.ppermute(send, 'freq', pairs)  1.92 us
  transfers between devices with their start and end apart: 9, of which 6 were waited for; matrix products, arithmetic and copies ran while one was open for 0% of the time, Pallas kernels for 1%

profile of v5, /device:TPU:384, one launch (start us, length us, event | category | flops | bytes accessed | tf_op | source)
XLA Modules:
  0.0 78.9 jit_solution(1507993834236489154)
XLA Ops:
  0.0 1.5 %shard_map.55 = (f32[5,128,128]{2,1,0:T(8,128)S(1)}, f32[4,128,128]{2,1,0:T(8,128)S(1)}, f32[10,128,128]{2,1,0:T(8,128)S(1)}, f32[3,128,128]{2,1,0:T(8,128)S(1)}...) custom-call(f32[1,2]{1,0:T(1,128)} %shifts_hbm.1, ...), custom_call_target="tpu_custom_call" | custom-call | flops 2000000 | bytes 2000000 | tf_op jit(solution)/shard_map/pallas_call | solution.py:334
  1.5 1.9 %collective-permute-start.2 = (f32[10,128,128]{2,1,0:T(8,128)S(1)}, f32[10,128,128]{2,1,0:T(8,128)S(1)}, u32[]{:S(2)}, u32[]{:S(2)}) collective-permute-start(f32[10,128,128]{2,1,0:T(8,128)S(1)} %get-tuple-element.29.own_b.own_b1), channel_id=1, source_target_pairs={{0,1},{1,0},{2,3},{3,2},{4,5},{5,4},{6,7},{7,6},{8,9},{9,8},{10,11... | collective-permute-start | bytes 1966088 | tf_op jit(solution)/shard_map/ppermute | solution.py:357
  3.5 6.4 %collective-permute-start = (f32[5,128,128]{2,1,0:T(8,128)S(1)}, f32[5,128,128]{2,1,0:T(8,128)S(1)}, u32[]{:S(2)}, u32[]{:S(2)}) collective-permute-start(f32[5,128,128]{2,1,0:T(8,128)S(1)} %get-tuple-element.27.own_a0.own_a1), channel_id=1, source_target_pairs={{1,2},{2,1},{3,4},{4,3},{5,6},{6,5},{7,8},{8,7},{9,10},{10,9},{11,... | collective-permute-start | bytes 983048 | tf_op jit(solution)/shard_map/ppermute | solution.py:350
  9.9 2.5 %collective-permute-start.1 = (f32[4,128,128]{2,1,0:T(8,128)S(1)}, f32[4,128,128]{2,1,0:T(8,128)S(1)}, u32[]{:S(2)}, u32[]{:S(2)}) collective-permute-start(f32[4,128,128]{2,1,0:T(8,128)S(1)} %get-tuple-element.28.own_a1), channel_id=1, source_target_pairs={{1,2},{2,1},{3,4},{4,3},{5,6},{6,5},{7,8},{8,7},{9,10},{10,9},{11,... | collective-permute-start | bytes 786440 | tf_op jit(solution)/shard_map/ppermute | solution.py:350
  12.4 2.8 %collective-permute-done.got_a0.got_a1.med_a = f32[5,128,128]{2,1,0:T(8,128)S(1)} collective-permute-done((f32[5,128,128]{2,1,0:T(8,128)S(1)}, f32[5,128,128]{2,1,0:T(8,128)S(1)}, u32[]{:S(2)}, u32[]{:S(2)}) %collective-permute-start) | collective-permute-done | bytes 327712 | tf_op jit(solution)/shard_map/ppermute | solution.py:350
  15.2 0.5 shard_map.56
  15.7 5.3 %collective-permute-done.1.got_a1 = f32[4,128,128]{2,1,0:T(8,128)S(1)} collective-permute-done((f32[4,128,128]{2,1,0:T(8,128)S(1)}, f32[4,128,128]{2,1,0:T(8,128)S(1)}, u32[]{:S(2)}, u32[]{:S(2)}) %collective-permute-start.1) | collective-permute-done | bytes 262176 | tf_op jit(solution)/shard_map/ppermute | solution.py:350
  20.9 0.5 shard_map.57
  21.4 1.9 %collective-permute-start.4 = (f32[8,128,128]{2,1,0:T(8,128)S(1)}, f32[8,128,128]{2,1,0:T(8,128)S(1)}, u32[]{:S(2)}, u32[]{:S(2)}) collective-permute-start(f32[8,128,128]{2,1,0:T(8,128)S(1)} %get-tuple-element.34.own_b), channel_id=1, source_target_pairs={{0,1},{1,0},{2,3},{3,2},{4,5},{5,4},{6,7},{7,6},{8,9},{9,8},{10,11... | collective-permute-start | bytes 1572872 | tf_op jit(solution)/shard_map/ppermute | solution.py:357
  23.3 3.5 %collective-permute-start.5 = (f32[7,128,128]{2,1,0:T(8,128)S(1)}, f32[7,128,128]{2,1,0:T(8,128)S(1)}, u32[]{:S(2)}, u32[]{:S(2)}) collective-permute-start(f32[7,128,128]{2,1,0:T(8,128)S(1)} %get-tuple-element.35.own_a), channel_id=1, source_target_pairs={{1,2},{2,1},{3,4},{4,3},{5,6},{6,5},{7,8},{8,7},{9,10},{10,9},{11,... | collective-permute-start | bytes 1376264 | tf_op jit(solution)/shard_map/ppermute | solution.py:350
  26.8 5.4 %collective-permute-start.3 = (f32[4,128,128]{2,1,0:T(8,128)S(1)}, f32[4,128,128]{2,1,0:T(8,128)S(1)}, u32[]{:S(2)}, u32[]{:S(2)}) collective-permute-start(f32[4,128,128]{2,1,0:T(8,128)S(1)} %get-tuple-element.33.own_a), channel_id=1, source_target_pairs={{1,2},{2,1},{3,4},{4,3},{5,6},{6,5},{7,8},{8,7},{9,10},{10,9},{11,... | collective-permute-start | bytes 786440 | tf_op jit(solution)/shard_map/ppermute | solution.py:350
  32.2 4.2 %collective-permute-done.5.got_a.got_a2 = f32[7,128,128]{2,1,0:T(8,128)S(1)} collective-permute-done((f32[7,128,128]{2,1,0:T(8,128)S(1)}, f32[7,128,128]{2,1,0:T(8,128)S(1)}, u32[]{:S(2)}, u32[]{:S(2)}) %collective-permute-start.5) | collective-permute-done | bytes 458784 | tf_op jit(solution)/shard_map/ppermute | solution.py:350
  36.4 0.5 shard_map.58
  36.9 2.3 %collective-permute-done.3.got_a = f32[4,128,128]{2,1,0:T(8,128)S(1)} collective-permute-done((f32[4,128,128]{2,1,0:T(8,128)S(1)}, f32[4,128,128]{2,1,0:T(8,128)S(1)}, u32[]{:S(2)}, u32[]{:S(2)}) %collective-permute-start.3) | collective-permute-done | bytes 262176 | tf_op jit(solution)/shard_map/ppermute | solution.py:350
  39.2 0.5 shard_map.59
  39.8 4.0 %collective-permute-start.6 = (f32[6,128,128]{2,1,0:T(8,128)S(1)}, f32[6,128,128]{2,1,0:T(8,128)S(1)}, u32[]{:S(2)}, u32[]{:S(2)}) collective-permute-start(f32[6,128,128]{2,1,0:T(8,128)S(1)} %get-tuple-element.38.own_a), channel_id=1, source_target_pairs={{1,2},{2,1},{3,4},{4,3},{5,6},{6,5},{7,8},{8,7},{9,10},{10,9},{11,... | collective-permute-start | bytes 1179656 | tf_op jit(solution)/shard_map/ppermute | solution.py:350
  43.8 1.9 %collective-permute-start.7 = (f32[6,128,128]{2,1,0:T(8,128)S(1)}, f32[6,128,128]{2,1,0:T(8,128)S(1)}, u32[]{:S(2)}, u32[]{:S(2)}) collective-permute-start(f32[6,128,128]{2,1,0:T(8,128)S(1)} %get-tuple-element.39.own_b), channel_id=1, source_target_pairs={{0,1},{1,0},{2,3},{3,2},{4,5},{5,4},{6,7},{7,6},{8,9},{9,8},{10,11... | collective-permute-start | bytes 1179656 | tf_op jit(solution)/shard_map/ppermute | solution.py:357
  45.7 6.5 %collective-permute-done.6.got_a = f32[6,128,128]{2,1,0:T(8,128)S(1)} collective-permute-done((f32[6,128,128]{2,1,0:T(8,128)S(1)}, f32[6,128,128]{2,1,0:T(8,128)S(1)}, u32[]{:S(2)}, u32[]{:S(2)}) %collective-permute-start.6) | collective-permute-done | bytes 393248 | tf_op jit(solution)/shard_map/ppermute | solution.py:350
  52.2 0.3 shard_map.60.rest_0_
  52.5 0.3 shard_map.61
  52.8 10.9 %all_to_all.5.arrived = f32[8,2,2,16,128]{4,3,2,1,0:T(8,128)S(1)} all-to-all(f32[8,2,2,16,128]{4,3,2,1,0:T(8,128)S(1)} %shard_map.61), channel_id=1, replica_groups={{0,128,256,384},{64,192,320,448},{1,129,257,385},{65,193,321,449},{2,13..., dimensions={0} | all-to-all | bytes 524288 | tf_op jit(solution)/shard_map/all_to_all | solution.py:375
  63.8 1.9 %collective-permute-start.8 = (f32[2,2,16,128]{3,2,1,0:T(8,128)S(1)}, f32[2,2,16,128]{3,2,1,0:T(8,128)S(1)}, u32[]{:S(2)}, u32[]{:S(2)}) collective-permute-start(f32[2,2,16,128]{3,2,1,0:T(8,128)S(1)} %get-tuple-element.46), channel_id=1, source_target_pairs={{0,64},{64,0},{128,192},{192,128},{256,320},{320,256},{384,448},{4... | collective-permute-start | bytes 98312 | tf_op jit(solution)/shard_map/ppermute | solution.py:381
  65.7 12.6 %collective-permute-done.8 = f32[2,2,16,128]{3,2,1,0:T(8,128)S(1)} collective-permute-done((f32[2,2,16,128]{3,2,1,0:T(8,128)S(1)}, f32[2,2,16,128]{3,2,1,0:T(8,128)S(1)}, u32[]{:S(2)}, u32[]{:S(2)}) %collective-permute-start.8) | collective-permute-done | bytes 32800 | tf_op jit(solution)/shard_map/ppermute | solution.py:381
  78.3 0.6 add.3
  (4 shorter events, 0.0 us)
Async XLA Ops:
  1.5 13.6 %collective-permute-start.2 = (f32[10,128,128]{2,1,0:T(8,128)S(1)}, f32[10,128,128]{2,1,0:T(8,128)S(1)}, u32[]{:S(2)}, u32[]{:S(2)}) collective-permute-start(f32[10,128,128]{2,1,0:T(8,128)S(1)} %get-tuple-element.29.own_b.own_b1), channel_id=1, source_target_pairs={{0,1},{1,0},{2,3},{3,2},{4,5},{5,4},{6,7},{7,6},{8,9},{9,8},{10,11... | collective-permute-start | bytes 1966088 | tf_op jit(solution)/shard_map/ppermute | solution.py:357
  3.5 11.7 %collective-permute-start = (f32[5,128,128]{2,1,0:T(8,128)S(1)}, f32[5,128,128]{2,1,0:T(8,128)S(1)}, u32[]{:S(2)}, u32[]{:S(2)}) collective-permute-start(f32[5,128,128]{2,1,0:T(8,128)S(1)} %get-tuple-element.27.own_a0.own_a1), channel_id=1, source_target_pairs={{1,2},{2,1},{3,4},{4,3},{5,6},{6,5},{7,8},{8,7},{9,10},{10,9},{11,... | collective-permute-start | bytes 983048 | tf_op jit(solution)/shard_map/ppermute | solution.py:350
  9.9 11.0 %collective-permute-start.1 = (f32[4,128,128]{2,1,0:T(8,128)S(1)}, f32[4,128,128]{2,1,0:T(8,128)S(1)}, u32[]{:S(2)}, u32[]{:S(2)}) collective-permute-start(f32[4,128,128]{2,1,0:T(8,128)S(1)} %get-tuple-element.28.own_a1), channel_id=1, source_target_pairs={{1,2},{2,1},{3,4},{4,3},{5,6},{6,5},{7,8},{8,7},{9,10},{10,9},{11,... | collective-permute-start | bytes 786440 | tf_op jit(solution)/shard_map/ppermute | solution.py:350
  21.4 15.0 %collective-permute-start.4 = (f32[8,128,128]{2,1,0:T(8,128)S(1)}, f32[8,128,128]{2,1,0:T(8,128)S(1)}, u32[]{:S(2)}, u32[]{:S(2)}) collective-permute-start(f32[8,128,128]{2,1,0:T(8,128)S(1)} %get-tuple-element.34.own_b), channel_id=1, source_target_pairs={{0,1},{1,0},{2,3},{3,2},{4,5},{5,4},{6,7},{7,6},{8,9},{9,8},{10,11... | collective-permute-start | bytes 1572872 | tf_op jit(solution)/shard_map/ppermute | solution.py:357
  23.3 13.1 %collective-permute-start.5 = (f32[7,128,128]{2,1,0:T(8,128)S(1)}, f32[7,128,128]{2,1,0:T(8,128)S(1)}, u32[]{:S(2)}, u32[]{:S(2)}) collective-permute-start(f32[7,128,128]{2,1,0:T(8,128)S(1)} %get-tuple-element.35.own_a), channel_id=1, source_target_pairs={{1,2},{2,1},{3,4},{4,3},{5,6},{6,5},{7,8},{8,7},{9,10},{10,9},{11,... | collective-permute-start | bytes 1376264 | tf_op jit(solution)/shard_map/ppermute | solution.py:350
  26.8 12.4 %collective-permute-start.3 = (f32[4,128,128]{2,1,0:T(8,128)S(1)}, f32[4,128,128]{2,1,0:T(8,128)S(1)}, u32[]{:S(2)}, u32[]{:S(2)}) collective-permute-start(f32[4,128,128]{2,1,0:T(8,128)S(1)} %get-tuple-element.33.own_a), channel_id=1, source_target_pairs={{1,2},{2,1},{3,4},{4,3},{5,6},{6,5},{7,8},{8,7},{9,10},{10,9},{11,... | collective-permute-start | bytes 786440 | tf_op jit(solution)/shard_map/ppermute | solution.py:350
  39.8 12.4 %collective-permute-start.6 = (f32[6,128,128]{2,1,0:T(8,128)S(1)}, f32[6,128,128]{2,1,0:T(8,128)S(1)}, u32[]{:S(2)}, u32[]{:S(2)}) collective-permute-start(f32[6,128,128]{2,1,0:T(8,128)S(1)} %get-tuple-element.38.own_a), channel_id=1, source_target_pairs={{1,2},{2,1},{3,4},{4,3},{5,6},{6,5},{7,8},{8,7},{9,10},{10,9},{11,... | collective-permute-start | bytes 1179656 | tf_op jit(solution)/shard_map/ppermute | solution.py:350
  43.8 8.4 %collective-permute-start.7 = (f32[6,128,128]{2,1,0:T(8,128)S(1)}, f32[6,128,128]{2,1,0:T(8,128)S(1)}, u32[]{:S(2)}, u32[]{:S(2)}) collective-permute-start(f32[6,128,128]{2,1,0:T(8,128)S(1)} %get-tuple-element.39.own_b), channel_id=1, source_target_pairs={{0,1},{1,0},{2,3},{3,2},{4,5},{5,4},{6,7},{7,6},{8,9},{9,8},{10,11... | collective-permute-start | bytes 1179656 | tf_op jit(solution)/shard_map/ppermute | solution.py:357
  63.8 14.5 %collective-permute-start.8 = (f32[2,2,16,128]{3,2,1,0:T(8,128)S(1)}, f32[2,2,16,128]{3,2,1,0:T(8,128)S(1)}, u32[]{:S(2)}, u32[]{:S(2)}) collective-permute-start(f32[2,2,16,128]{3,2,1,0:T(8,128)S(1)} %get-tuple-element.46), channel_id=1, source_target_pairs={{0,64},{64,0},{128,192},{192,128},{256,320},{320,256},{384,448},{4... | collective-permute-start | bytes 98312 | tf_op jit(solution)/shard_map/ppermute | solution.py:381
